TPU v7x, 32 devices: a whole 2x2x4 slice. The times are simulated.
32 devices in a mesh: curve: 8 (over z, y), seg: 4 (over x, core).
Axes of the slice: x: 2, y: 2, z: 4, core: 2. Of those that a mesh axis runs over, the one named last changes fastest.
Arguments:
- solution: bfloat16 [16384, 128], P(('curve', 'seg')), may hold values from -6 to 6
- viscosity: float32 [131072], P(('curve', 'seg')), may hold values from 0.1 to 10
- slot_index: int32 [131072, 4], P(('curve', 'seg')), may hold values from 0 to 1279, as said below
- slot_weight: int32 [131072, 4], P(('curve', 'seg')), may hold values from -1 to 8, as said below
- mirror_rows: int32 [32, 4, 192], P(('curve', 'seg')), may hold values from 0 to 511
- ghost_live: int32 [32, 4], P(('curve', 'seg')), may hold values from 0 to 192, as said below
- cell_count: int32 [32], P(('curve', 'seg')), may hold values from 512 to 4096, as said below
- viscous_block: bfloat16 [128, 128], replicated, may hold values from -0.5 to 0.5
- pressure_block: bfloat16 [128, 128], replicated, may hold values from -0.5 to 0.5
Outputs:
- residual: float32 [16384, 128], P(('curve', 'seg'))
Inputs may be any that keep to these rules, and one draw needn't show every extreme that they name: `slot_index`: column 0 of each element is one of its device's owned blocks; other columns point to owned blocks or to ghost entries; ghost entries past a list's live count read zeros. `slot_weight`: each entry is one of -1, 3, 6, 8; column 0 is 8. `ghost_live`: some list is full in every draw. `cell_count`: some device is full in every draw; loads are skewed.
All inputs are finite; a program needn't handle non-finite values.
Results may differ from a plain program's by a relative error of at most 0.0035.
Values may be sent and summed in bfloat16 or wider, within the bound.
No kernel may reach another device: no remote copies, remote signals or barrier semaphores. Data moves between devices by JAX's collectives and lax.ppermute only.
A program may use at most 64 MiB of HBM per device.

v0:
```python
import functools

import jax
import jax.numpy as jnp
from jax import lax
from jax.experimental import pallas as pl
from jax.experimental.pallas import tpu as pltpu
from jax.sharding import PartitionSpec as P

AXES = ("curve", "seg")
PACK = 16
VMEM = pl.BlockSpec(memory_space=pltpu.VMEM)
SMEM = pl.BlockSpec(memory_space=pltpu.SMEM)
HBM = pl.BlockSpec(memory_space=pltpu.HBM)


def matchings(region_count):
    return [(reach + 1, parity) for reach in range(region_count // 2) for parity in (0, 1)]


def exchange(block, distance, parity):
    total = lax.axis_size(AXES)
    route = []
    for d in range(total - distance):
        if (d // distance) % 2 == parity:
            route += [(d, d + distance), (d + distance, d)]
    return lax.ppermute(block, AXES, route)


def send_region(distance, parity):
    me = lax.axis_index("curve") * lax.axis_size("seg") + lax.axis_index("seg")
    up = (lax.div(me, distance) + parity) % 2
    return 2 * (distance - 1) + up


def transposed(values):
    return values.astype(jnp.float32).T.astype(jnp.bfloat16)


def matmul(a, b):
    return jnp.dot(a, b, preferred_element_type=jnp.float32)


def matmul_nt(a, b):
    return lax.dot_general(a, b, (((1,), (1,)), ((), ())), preferred_element_type=jnp.float32)


def one_hot(names, rows):
    wide = jnp.broadcast_to(names, (PACK, names.shape[1])).astype(jnp.int16)
    iota = lax.broadcasted_iota(jnp.int32, wide.shape, 0)
    one, zero = jnp.ones(wide.shape, jnp.bfloat16), jnp.zeros(wide.shape, jnp.bfloat16)
    return jnp.concatenate([jnp.where(wide == (iota + g * PACK).astype(jnp.int16), one, zero) for g in range(rows // PACK)], axis=0)


def select_kernel(pairs, loads, mirror_hbm, live_hbm, sol_hbm, *rest):
    n = len(pairs)
    load_refs, rest = rest[:loads], rest[loads:]
    sent_refs, (names_ref, flipped_ref), rest = rest[:n], rest[n : n + 2], rest[n + 2 :]
    copy_refs, (mirror_ref, live_ref, sol_ref, sems) = rest[:loads], rest[loads:]
    first = [
        pltpu.make_async_copy(src, dst, sems.at[i])
        for i, (src, dst) in enumerate(((sol_hbm, sol_ref), (mirror_hbm, mirror_ref), (live_hbm, live_ref)))
    ]
    later = [pltpu.make_async_copy(src, dst, sems.at[len(first) + i]) for i, (src, dst) in enumerate(zip(load_refs, copy_refs))]
    for copy in first + later:
        copy.start()
    for copy in first:
        copy.wait()
    rows, ghost = sol_ref.shape[0], mirror_ref.shape[2]
    flipped = transposed(sol_ref[...])
    flipped_ref[...] = flipped
    lane = lax.broadcasted_iota(jnp.int32, (1, ghost), 1)
    for m, (distance, parity) in enumerate(pairs):
        region = send_region(distance, parity)
        names = jnp.where(lane < live_ref[0, region], mirror_ref[0, pl.ds(region, 1), :], -1)
        names_ref[pl.ds(m, 1), :] = names
        sent_refs[m][...] = matmul(flipped, one_hot(names, rows)).T.astype(jnp.bfloat16)
    for copy in later:
        copy.wait()


def slot_rows(index_ref, weight_ref, count_ref, start, width):
    slots = index_ref.shape[0]
    lanes = pl.ds(start, width)
    live = lax.broadcasted_iota(jnp.int32, (1, width), 1) + start < count_ref[0]
    names = [index_ref[pl.ds(i, 1), lanes] for i in range(slots)]
    codes = [weight_ref[pl.ds(i, 1), lanes] for i in range(slots)]
    sums = list(codes)
    for i in range(slots):
        for j in range(i + 1, slots):
            sums[i] = sums[i] + jnp.where(names[i] == names[j], codes[j], 0)
    out = []
    for i in range(slots):
        scaled = jnp.where(live, sums[i].astype(jnp.float32) * 0.125, 0.0)
        column = jnp.broadcast_to(names[i], (PACK, width)).astype(jnp.int16)
        weight = jnp.broadcast_to(scaled, (PACK, width)).astype(jnp.bfloat16)
        out.append((column, weight))
    return out


def selection(slots, base, rows, width):
    iota = lax.broadcasted_iota(jnp.int32, (PACK, width), 0)
    pieces = []
    for g in range(rows // PACK):
        here = (iota + (base + g * PACK)).astype(jnp.int16)
        piece = jnp.zeros((PACK, width), jnp.bfloat16)
        for column, weight in reversed(slots):
            piece = jnp.where(column == here, weight, piece)
        pieces.append(piece)
    return jnp.concatenate(pieces, axis=0)


def over_blocks(total, width, unroll, step):
    group = width * unroll

    def body(b, carry):
        for u in range(unroll):
            step(pl.multiple_of(b * group + u * width, width))
        return carry

    lax.fori_loop(0, total // group, body, 0)


def gather_kernel(width, unroll, count_ref, index_ref, weight_ref, flipped_ref, ein_ref, table_ref, turned_ref):
    owned, columns = flipped_ref.shape[1], table_ref.shape[0]

    def step(start):
        lanes = pl.ds(start, width)
        slots = slot_rows(index_ref, weight_ref, count_ref, start, width)
        ein_ref[:, lanes] = matmul(flipped_ref[...], selection(slots, 0, owned, width))
        table = selection(slots[1:], owned, columns, width)
        table_ref[:, lanes] = table
        turned_ref[lanes, :] = table.T

    over_blocks(ein_ref.shape[1], width, unroll, step)


def element_kernel(width, unroll, pairs, visc_ref, ein_ref, table_ref, turned_ref, mats_v_ref, mats_p_ref, *rest):
    n = len(pairs)
    ghost_refs, out_ref, ret_refs, (ghost_all, total, back) = rest[:n], rest[n], rest[n + 1 : 2 * n + 1], rest[2 * n + 1 :]
    ghost = ghost_refs[0].shape[0]
    spots = []
    for (distance, parity), ghost_ref in zip(pairs, ghost_refs):
        sent = send_region(distance, parity)
        got = 4 * (distance - 1) + 1 - sent
        spot = pl.ds(pl.multiple_of(got * ghost, PACK), ghost)
        spots.append(spot)
        ghost_all[spot, :] = ghost_ref[...]
    flipped = transposed(ghost_all[...])
    both = jnp.concatenate([mats_v_ref[...].astype(jnp.float32).T, mats_p_ref[...].astype(jnp.float32).T], axis=1).astype(jnp.bfloat16)
    total[...] = jnp.zeros_like(total)

    def step(start):
        lanes = pl.ds(start, width)
        ein = ein_ref[:, lanes] + matmul(flipped, table_ref[:, lanes])
        stacked = jnp.concatenate([ein * visc_ref[:, lanes], ein], axis=0).astype(jnp.bfloat16)
        out = matmul(both, stacked).astype(jnp.bfloat16)
        out_ref[:, lanes] = out
        total[...] += matmul(out, turned_ref[lanes, :])

    over_blocks(ein_ref.shape[1], width, unroll, step)
    back[...] = total[...].T
    for spot, ret_ref in zip(spots, ret_refs):
        ret_ref[...] = back[spot, :].astype(jnp.bfloat16)


def scatter_kernel(width, unroll, count_ref, index_ref, weight_ref, out_ref, names_ref, part_ref, *hit_refs):
    owned = part_ref.shape[0]
    part_ref[...] = jnp.zeros_like(part_ref)
    for m, hit_ref in enumerate(hit_refs):
        hit_ref[...] = one_hot(names_ref[pl.ds(m, 1), :], owned)

    def step(start):
        lanes = pl.ds(start, width)
        slots = slot_rows(index_ref, weight_ref, count_ref, start, width)
        part_ref[...] += matmul_nt(selection(slots, 0, owned, width), out_ref[:, lanes])

    over_blocks(out_ref.shape[1], width, unroll, step)


def finish_kernel(n, part_ref, *rest):
    hit_refs, back_refs, res_ref = rest[:n], rest[n : 2 * n], rest[2 * n]
    total = part_ref[...]
    for hit_ref, back_ref in zip(hit_refs, back_refs):
        total = total + matmul(hit_ref[...], back_ref[...])
    res_ref[...] = total


def params(limit):
    return pltpu.CompilerParams(vmem_limit_bytes=limit * 1024 * 1024)


def cost(flops):
    return pl.CostEstimate(flops=flops, bytes_accessed=1 << 20, transcendentals=0)


def like(*arrays):
    return [jax.ShapeDtypeStruct(a.shape, a.dtype) for a in arrays]


def per_device(
    solution,
    viscosity,
    slot_index,
    slot_weight,
    mirror_rows,
    ghost_live,
    cell_count,
    viscous_block,
    pressure_block,
):
    owned, channels = solution.shape
    regions, ghost = mirror_rows.shape[1:]
    elements = viscosity.shape[0]
    width = min(512, elements)
    unroll = min(4, elements // width)
    pairs = matchings(regions)
    bf16, f32 = jnp.bfloat16, jnp.float32
    table_flops = 2 * elements * channels
    list_shape = [jax.ShapeDtypeStruct((ghost, channels), bf16)] * regions
    loads = [slot_index.T, slot_weight.T, viscosity.reshape(1, elements), viscous_block, pressure_block]

    outs = pl.pallas_call(
        functools.partial(select_kernel, pairs, len(loads)),
        out_shape=list_shape
        + [
            jax.ShapeDtypeStruct((regions, ghost), jnp.int32),
            jax.ShapeDtypeStruct((channels, owned), bf16),
        ]
        + like(*loads),
        in_specs=[HBM] * (3 + len(loads)),
        out_specs=[VMEM] * (regions + 2 + len(loads)),
        scratch_shapes=[
            pltpu.VMEM(mirror_rows.shape, jnp.int32),
            pltpu.SMEM(ghost_live.shape, jnp.int32),
            pltpu.VMEM(solution.shape, bf16),
            pltpu.SemaphoreType.DMA((3 + len(loads),)),
        ],
        compiler_params=params(16),
        cost_estimate=cost(2 * owned * channels * regions * ghost),
        name="select",
    )(*[pltpu.with_memory_space_constraint(a, pltpu.HBM) for a in (mirror_rows, ghost_live, solution, *loads)])
    sent, (names, flipped, index, weight, visc, mats_v, mats_p) = outs[:regions], outs[regions:]
    got = [exchange(block, *pair) for block, pair in zip(sent, pairs)]

    ein, table, turned = pl.pallas_call(
        functools.partial(gather_kernel, width, unroll),
        out_shape=[
            jax.ShapeDtypeStruct((channels, elements), f32),
            jax.ShapeDtypeStruct((regions * ghost, elements), bf16),
            jax.ShapeDtypeStruct((elements, regions * ghost), bf16),
        ],
        in_specs=[SMEM] + [VMEM] * 3,
        out_specs=[VMEM] * 3,
        compiler_params=params(20),
        cost_estimate=cost(table_flops * owned * 8),
        name="gather_owned",
    )(cell_count, index, weight, flipped)

    out, *ret = pl.pallas_call(
        functools.partial(element_kernel, width, unroll, pairs),
        out_shape=[jax.ShapeDtypeStruct((channels, elements), bf16)] + list_shape,
        in_specs=[VMEM] * (6 + regions),
        out_specs=[VMEM] * (1 + regions),
        scratch_shapes=[
            pltpu.VMEM((regions * ghost, channels), bf16),
            pltpu.VMEM((channels, regions * ghost), f32),
            pltpu.VMEM((regions * ghost, channels), f32),
        ],
        compiler_params=params(20),
        cost_estimate=cost(table_flops * regions * ghost * 2),
        name="elements",
    )(visc, ein, table, turned, mats_v, mats_p, *got)
    back = [exchange(block, *pair) for block, pair in zip(ret, pairs)]

    part, *hits = pl.pallas_call(
        functools.partial(scatter_kernel, width, unroll),
        out_shape=[jax.ShapeDtypeStruct((owned, channels), f32)] + [jax.ShapeDtypeStruct((owned, ghost), bf16)] * regions,
        in_specs=[SMEM] + [VMEM] * 4,
        out_specs=[VMEM] * (1 + regions),
        compiler_params=params(20),
        cost_estimate=cost(table_flops * owned * 8),
        name="scatter_owned",
    )(cell_count, index, weight, out, names)

    return pl.pallas_call(
        functools.partial(finish_kernel, regions),
        out_shape=jax.ShapeDtypeStruct((owned, channels), f32),
        in_specs=[VMEM] * (1 + 2 * regions),
        out_specs=VMEM,
        compiler_params=params(16),
        cost_estimate=cost(2 * owned * channels * regions * ghost),
        name="finish",
    )(part, *hits, *back)


def solution(mesh):
    return jax.shard_map(
        per_device,
        mesh=mesh,
        in_specs=(
            P(AXES, None),
            P(AXES),
            P(AXES, None),
            P(AXES, None),
            P(AXES, None, None),
            P(AXES, None),
            P(AXES),
            P(),
            P(),
        ),
        out_specs=P(AXES, None),
        check_vma=False,
    )
```

profile of v0, /device:TPU:17, one launch (start us, length us, event | category | flops | bytes accessed | tf_op | source)
XLA Modules:
  0.0 32.0 jit_solution(10450534358173970948)
XLA Ops:
  0.0 1.4 %select.1 = (bf16[192,128]{1,0:T(8,128)(2,1)S(1)}, bf16[192,128]{1,0:T(8,128)(2,1)S(1)}, bf16[192,128]{1,0:T(8,128)(2,1)S(1)}, bf16[192,128]{1,0:T(8,128)(2,1)S(...) custom-call(s32[1,4,192]{2,1,0:T(4,128)} %mirror_hbm.1, ...), custom_call_target="tpu_custom_call" | custom-call | flops 100663296 | bytes 1048576 | tf_op jit(solution)/shard_map/select/pallas_call | solution.py:223
  1.4 0.7 %collective-permute-start = (bf16[192,128]{1,0:T(8,128)(2,1)S(1)}, bf16[192,128]{1,0:T(8,128)(2,1)S(1)}, u32[]{:S(2)}, u32[]{:S(2)}) collective-permute-start(bf16[192,128]{1,0:T(8,128)(2,1)S(1)} %get-tuple-element.38), channel_id=1, source_target_pairs={{0,1},{1,0},{2,3},{3,2},{4,5},{5,4},{6,7},{7,6},{8,9},{9,8},{10,11... | collective-permute-start | bytes 147464 | tf_op jit(solution)/shard_map/ppermute | solution.py:27
  2.2 3.0 %collective-permute-start.1 = (bf16[192,128]{1,0:T(8,128)(2,1)S(1)}, bf16[192,128]{1,0:T(8,128)(2,1)S(1)}, u32[]{:S(2)}, u32[]{:S(2)}) collective-permute-start(bf16[192,128]{1,0:T(8,128)(2,1)S(1)} %get-tuple-element.39), channel_id=1, source_target_pairs={{1,2},{2,1},{3,4},{4,3},{5,6},{6,5},{7,8},{8,7},{9,10},{10,9},{11,... | collective-permute-start | bytes 147464 | tf_op jit(solution)/shard_map/ppermute | solution.py:27
  5.2 1.3 %collective-permute-start.2 = (bf16[192,128]{1,0:T(8,128)(2,1)S(1)}, bf16[192,128]{1,0:T(8,128)(2,1)S(1)}, u32[]{:S(2)}, u32[]{:S(2)}) collective-permute-start(bf16[192,128]{1,0:T(8,128)(2,1)S(1)} %get-tuple-element.40), channel_id=1, source_target_pairs={{0,2},{2,0},{1,3},{3,1},{4,6},{6,4},{5,7},{7,5},{8,10},{10,8},{9,1... | collective-permute-start | bytes 147464 | tf_op jit(solution)/shard_map/ppermute | solution.py:27
  6.5 3.0 %collective-permute-start.3 = (bf16[192,128]{1,0:T(8,128)(2,1)S(1)}, bf16[192,128]{1,0:T(8,128)(2,1)S(1)}, u32[]{:S(2)}, u32[]{:S(2)}) collective-permute-start(bf16[192,128]{1,0:T(8,128)(2,1)S(1)} %get-tuple-element.41), channel_id=1, source_target_pairs={{2,4},{4,2},{3,5},{5,3},{6,8},{8,6},{7,9},{9,7},{10,12},{12,10},{1... | collective-permute-start | bytes 147464 | tf_op jit(solution)/shard_map/ppermute | solution.py:27
  10.1 3.5 %gather_owned.1 = (f32[128,4096]{1,0:T(8,128)S(1)}, bf16[768,4096]{1,0:T(8,128)(2,1)S(1)}, bf16[4096,768]{1,0:T(8,128)(2,1)S(1)}) custom-call(s32[1]{0:T(128)S(6)} %copy.10.count_ref, s32[4,4096]{1,0:T(4,128)S(1)} %get-tuple-element.29.index_ref, s32[4,4096]{1,0:T(4,128)S(1)} %get-tuple-element.30.weight_ref, bf16[128,512]{1,0:T(8,128)(2,1)S(1)} %get-tuple-element.32.flipped_ref), custom_call_target="tpu_custom_call" | custom-call | flops 4294967296 | bytes 1048576 | tf_op jit(solution)/shard_map/gather_owned/pallas_call | solution.py:246
  13.6 0.0 collective-permute-done.rest_0_
  13.6 0.0 collective-permute-done.1.rest_1_
  13.6 0.0 collective-permute-done.2.rest_2_
  13.6 0.0 collective-permute-done.3.rest_3_
  13.6 4.7 %elements.1 = (bf16[128,4096]{1,0:T(8,128)(2,1)S(1)}, bf16[192,128]{1,0:T(8,128)(2,1)S(1)}, bf16[192,128]{1,0:T(8,128)(2,1)S(1)}, bf16[192,128]{1,0:T(8,128)(2,1)S(1)}, bf16[192,128]{1,0:T(8,128)(2,1)S(1)}) custom-call(f32[1,4096]{1,0:T(1,128)S(1)} %get-tuple-element.31.visc_ref, f32[128,4096]{1,0:T(8,128)S(1)} %get-tuple-element.33.ein_ref, ...), custom_call_target="tpu_custom_call" | custom-call | flops 1610612736 | bytes 1048576 | tf_op jit(solution)/shard_map/elements/pallas_call | solution.py:260
  18.3 1.1 %collective-permute-start.4 = (bf16[192,128]{1,0:T(8,128)(2,1)S(1)}, bf16[192,128]{1,0:T(8,128)(2,1)S(1)}, u32[]{:S(2)}, u32[]{:S(2)}) collective-permute-start(bf16[192,128]{1,0:T(8,128)(2,1)S(1)} %get-tuple-element.49), channel_id=1, source_target_pairs={{0,1},{1,0},{2,3},{3,2},{4,5},{5,4},{6,7},{7,6},{8,9},{9,8},{10,11... | collective-permute-start | bytes 147464 | tf_op jit(solution)/shard_map/ppermute | solution.py:27
  19.4 2.6 %collective-permute-start.5 = (bf16[192,128]{1,0:T(8,128)(2,1)S(1)}, bf16[192,128]{1,0:T(8,128)(2,1)S(1)}, u32[]{:S(2)}, u32[]{:S(2)}) collective-permute-start(bf16[192,128]{1,0:T(8,128)(2,1)S(1)} %get-tuple-element.50), channel_id=1, source_target_pairs={{1,2},{2,1},{3,4},{4,3},{5,6},{6,5},{7,8},{8,7},{9,10},{10,9},{11,... | collective-permute-start | bytes 147464 | tf_op jit(solution)/shard_map/ppermute | solution.py:27
  22.0 1.7 %collective-permute-start.6 = (bf16[192,128]{1,0:T(8,128)(2,1)S(1)}, bf16[192,128]{1,0:T(8,128)(2,1)S(1)}, u32[]{:S(2)}, u32[]{:S(2)}) collective-permute-start(bf16[192,128]{1,0:T(8,128)(2,1)S(1)} %get-tuple-element.51), channel_id=1, source_target_pairs={{0,2},{2,0},{1,3},{3,1},{4,6},{6,4},{5,7},{7,5},{8,10},{10,8},{9,1... | collective-permute-start | bytes 147464 | tf_op jit(solution)/shard_map/ppermute | solution.py:27
  23.7 2.8 %collective-permute-start.7 = (bf16[192,128]{1,0:T(8,128)(2,1)S(1)}, bf16[192,128]{1,0:T(8,128)(2,1)S(1)}, u32[]{:S(2)}, u32[]{:S(2)}) collective-permute-start(bf16[192,128]{1,0:T(8,128)(2,1)S(1)} %get-tuple-element.52), channel_id=1, source_target_pairs={{2,4},{4,2},{3,5},{5,3},{6,8},{8,6},{7,9},{9,7},{10,12},{12,10},{1... | collective-permute-start | bytes 147464 | tf_op jit(solution)/shard_map/ppermute | solution.py:27
  26.4 1.7 %scatter_owned.1 = (f32[512,128]{1,0:T(8,128)S(1)}, bf16[512,192]{1,0:T(8,128)(2,1)S(1)}, bf16[512,192]{1,0:T(8,128)(2,1)S(1)}, bf16[512,192]{1,0:T(8,128)(2,1)S(1)}, bf16[512,192]{1,0:T(8,128)(2,1)S(1)}) custom-call(s32[1]{0:T(128)S(6)} %copy.10.count_ref, s32[4,4096]{1,0:T(4,128)S(1)} %get-tuple-element.29.index_ref, ...), custom_call_target="tpu_custom_call" | custom-call | flops 4294967296 | bytes 1048576 | tf_op jit(solution)/shard_map/scatter_owned/pallas_call | solution.py:276
  28.2 0.0 collective-permute-done.4.rest_4_
  28.2 0.0 collective-permute-done.5.rest_5_
  28.2 0.0 collective-permute-done.6.rest_6_
  28.2 2.7 %collective-permute-done.7.rest_7_ = bf16[192,128]{1,0:T(8,128)(2,1)S(1)} collective-permute-done((bf16[192,128]{1,0:T(8,128)(2,1)S(1)}, bf16[192,128]{1,0:T(8,128)(2,1)S(1)}, u32[]{:S(2)}, u32[]{:S(2)}) %collective-permute-start.7) | collective-permute-done | bytes 49184 | tf_op jit(solution)/shard_map/ppermute | solution.py:27
  30.9 1.1 %finish.1 = f32[512,128]{1,0:T(8,128)} custom-call(f32[512,128]{1,0:T(8,128)S(1)} %get-tuple-element.44.part_ref, bf16[512,192]{1,0:T(8,128)(2,1)S(1)} %get-tuple-element.45.rest_0_, bf16[512,192]{1,0:T(8,128)(2,1)S(1)} %get-tuple-element.46.rest_1_, bf16[512,192]{1,0:T(8,128)(2,1)S(1)} %get-tuple-element.47.rest_2_, ...), custom_call_target="tpu_custom_call" | custom-call | flops 100663296 | bytes 1048576 | tf_op jit(solution)/shard_map/finish/pallas_call | solution.py:286
Async XLA Ops:
  1.4 12.2 %collective-permute-start = (bf16[192,128]{1,0:T(8,128)(2,1)S(1)}, bf16[192,128]{1,0:T(8,128)(2,1)S(1)}, u32[]{:S(2)}, u32[]{:S(2)}) collective-permute-start(bf16[192,128]{1,0:T(8,128)(2,1)S(1)} %get-tuple-element.38), channel_id=1, source_target_pairs={{0,1},{1,0},{2,3},{3,2},{4,5},{5,4},{6,7},{7,6},{8,9},{9,8},{10,11... | collective-permute-start | bytes 147464 | tf_op jit(solution)/shard_map/ppermute | solution.py:27
  2.2 11.4 %collective-permute-start.1 = (bf16[192,128]{1,0:T(8,128)(2,1)S(1)}, bf16[192,128]{1,0:T(8,128)(2,1)S(1)}, u32[]{:S(2)}, u32[]{:S(2)}) collective-permute-start(bf16[192,128]{1,0:T(8,128)(2,1)S(1)} %get-tuple-element.39), channel_id=1, source_target_pairs={{1,2},{2,1},{3,4},{4,3},{5,6},{6,5},{7,8},{8,7},{9,10},{10,9},{11,... | collective-permute-start | bytes 147464 | tf_op jit(solution)/shard_map/ppermute | solution.py:27
  5.2 8.4 %collective-permute-start.2 = (bf16[192,128]{1,0:T(8,128)(2,1)S(1)}, bf16[192,128]{1,0:T(8,128)(2,1)S(1)}, u32[]{:S(2)}, u32[]{:S(2)}) collective-permute-start(bf16[192,128]{1,0:T(8,128)(2,1)S(1)} %get-tuple-element.40), channel_id=1, source_target_pairs={{0,2},{2,0},{1,3},{3,1},{4,6},{6,4},{5,7},{7,5},{8,10},{10,8},{9,1... | collective-permute-start | bytes 147464 | tf_op jit(solution)/shard_map/ppermute | solution.py:27
  6.5 7.2 %collective-permute-start.3 = (bf16[192,128]{1,0:T(8,128)(2,1)S(1)}, bf16[192,128]{1,0:T(8,128)(2,1)S(1)}, u32[]{:S(2)}, u32[]{:S(2)}) collective-permute-start(bf16[192,128]{1,0:T(8,128)(2,1)S(1)} %get-tuple-element.41), channel_id=1, source_target_pairs={{2,4},{4,2},{3,5},{5,3},{6,8},{8,6},{7,9},{9,7},{10,12},{12,10},{1... | collective-permute-start | bytes 147464 | tf_op jit(solution)/shard_map/ppermute | solution.py:27
  18.3 9.9 %collective-permute-start.4 = (bf16[192,128]{1,0:T(8,128)(2,1)S(1)}, bf16[192,128]{1,0:T(8,128)(2,1)S(1)}, u32[]{:S(2)}, u32[]{:S(2)}) collective-permute-start(bf16[192,128]{1,0:T(8,128)(2,1)S(1)} %get-tuple-element.49), channel_id=1, source_target_pairs={{0,1},{1,0},{2,3},{3,2},{4,5},{5,4},{6,7},{7,6},{8,9},{9,8},{10,11... | collective-permute-start | bytes 147464 | tf_op jit(solution)/shard_map/ppermute | solution.py:27
  19.4 8.8 %collective-permute-start.5 = (bf16[192,128]{1,0:T(8,128)(2,1)S(1)}, bf16[192,128]{1,0:T(8,128)(2,1)S(1)}, u32[]{:S(2)}, u32[]{:S(2)}) collective-permute-start(bf16[192,128]{1,0:T(8,128)(2,1)S(1)} %get-tuple-element.50), channel_id=1, source_target_pairs={{1,2},{2,1},{3,4},{4,3},{5,6},{6,5},{7,8},{8,7},{9,10},{10,9},{11,... | collective-permute-start | bytes 147464 | tf_op jit(solution)/shard_map/ppermute | solution.py:27
  22.0 6.2 %collective-permute-start.6 = (bf16[192,128]{1,0:T(8,128)(2,1)S(1)}, bf16[192,128]{1,0:T(8,128)(2,1)S(1)}, u32[]{:S(2)}, u32[]{:S(2)}) collective-permute-start(bf16[192,128]{1,0:T(8,128)(2,1)S(1)} %get-tuple-element.51), channel_id=1, source_target_pairs={{0,2},{2,0},{1,3},{3,1},{4,6},{6,4},{5,7},{7,5},{8,10},{10,8},{9,1... | collective-permute-start | bytes 147464 | tf_op jit(solution)/shard_map/ppermute | solution.py:27
  23.7 7.2 %collective-permute-start.7 = (bf16[192,128]{1,0:T(8,128)(2,1)S(1)}, bf16[192,128]{1,0:T(8,128)(2,1)S(1)}, u32[]{:S(2)}, u32[]{:S(2)}) collective-permute-start(bf16[192,128]{1,0:T(8,128)(2,1)S(1)} %get-tuple-element.52), channel_id=1, source_target_pairs={{2,4},{4,2},{3,5},{5,3},{6,8},{8,6},{7,9},{9,7},{10,12},{12,10},{1... | collective-permute-start | bytes 147464 | tf_op jit(solution)/shard_map/ppermute | solution.py:27
where the time goes:
time: 32.2 us; the launch traced here: 32 us
  starting transfers between devices  16.1 us (50%)
  Pallas kernels  12.4 us (39%)
  waiting for transfers between devices  2.67 us (8%)
  between operations  0.76 us (2%)
    ppermute x8, starting transfers between devices, exchange(): return lax.ppermute(block, AXES, route)  16.1 us
    pallas_call x1, Pallas kernels, per_device(): pl.pallas_call(functools.partial(element_kernel, width, unroll, pairs), o...  4.67 us
    pallas_call x1, Pallas kernels, per_device(): pl.pallas_call(functools.partial(gather_kernel, width, unroll), out_shape...  3.47 us
    ppermute x8, waiting for transfers between devices, exchange(): return lax.ppermute(block, AXES, route)  2.67 us
    pallas_call x1, Pallas kernels, per_device(): pl.pallas_call(functools.partial(scatter_kernel, width, unroll), out_shap...  1.72 us
    pallas_call x1, Pallas kernels, per_device(): pl.pallas_call(functools.partial(select_kernel, pairs, len(loads)), out_s...  1.42 us
    pallas_call x1, Pallas kernels, per_device(): pl.pallas_call(functools.partial(finish_kernel, regions), out_shape=jax.S...  1.13 us
  transfers between devices with their start and end apart: 8, of which 1 were waited for; matrix products, arithmetic and copies ran while one was open for 0% of the time, Pallas kernels for 16%

commit v1 on v0

--- a/solution.py
+++ b/solution.py
@@ -15,7 +15,7 @@
 
 
 def matchings(region_count):
-    return [(reach + 1, parity) for reach in range(region_count // 2) for parity in (0, 1)]
+    return [(reach + 1, parity) for parity in (1, 0) for reach in reversed(range(region_count // 2))]
 
 
 def exchange(block, distance, parity):
@@ -79,10 +79,9 @@
         copy.wait()
 
 
-def slot_rows(index_ref, weight_ref, count_ref, start, width):
-    slots = index_ref.shape[0]
-    lanes = pl.ds(start, width)
-    live = lax.broadcasted_iota(jnp.int32, (1, width), 1) + start < count_ref[0]
+def slot_rows(index_ref, weight_ref, count, lanes):
+    slots, width = index_ref.shape[0], lanes.size
+    live = lax.broadcasted_iota(jnp.int32, (1, width), 1) + lanes.start < count
     names = [index_ref[pl.ds(i, 1), lanes] for i in range(slots)]
     codes = [weight_ref[pl.ds(i, 1), lanes] for i in range(slots)]
     sums = list(codes)
@@ -98,47 +97,49 @@
     return out
 
 
-def selection(slots, base, rows, width):
-    iota = lax.broadcasted_iota(jnp.int32, (PACK, width), 0)
+def load_rows(column_ref, share_ref, lanes, first):
+    slots = column_ref.shape[0] // PACK
+    return [(column_ref[i * PACK : (i + 1) * PACK, lanes], share_ref[i * PACK : (i + 1) * PACK, lanes]) for i in range(first, slots)]
+
+
+def selection(slots, base, rows):
+    shape = slots[0][0].shape
+    iota = lax.broadcasted_iota(jnp.int32, shape, 0)
     pieces = []
     for g in range(rows // PACK):
         here = (iota + (base + g * PACK)).astype(jnp.int16)
-        piece = jnp.zeros((PACK, width), jnp.bfloat16)
+        piece = jnp.zeros(shape, jnp.bfloat16)
         for column, weight in reversed(slots):
             piece = jnp.where(column == here, weight, piece)
         pieces.append(piece)
     return jnp.concatenate(pieces, axis=0)
 
 
-def over_blocks(total, width, unroll, step):
-    group = width * unroll
-
-    def body(b, carry):
-        for u in range(unroll):
-            step(pl.multiple_of(b * group + u * width, width))
-        return carry
-
-    lax.fori_loop(0, total // group, body, 0)
-
-
-def gather_kernel(width, unroll, count_ref, index_ref, weight_ref, flipped_ref, ein_ref, table_ref, turned_ref):
+def lane_blocks(total, width):
+    return [pl.ds(start, width) for start in range(0, total, width)]
+
+
+def gather_kernel(width, count_ref, index_ref, weight_ref, flipped_ref, ein_ref, column_ref, share_ref, table_ref, turned_ref):
     owned, columns = flipped_ref.shape[1], table_ref.shape[0]
-
-    def step(start):
-        lanes = pl.ds(start, width)
-        slots = slot_rows(index_ref, weight_ref, count_ref, start, width)
-        ein_ref[:, lanes] = matmul(flipped_ref[...], selection(slots, 0, owned, width))
-        table = selection(slots[1:], owned, columns, width)
-        table_ref[:, lanes] = table
-        turned_ref[lanes, :] = table.T
-
-    over_blocks(ein_ref.shape[1], width, unroll, step)
-
-
-def element_kernel(width, unroll, pairs, visc_ref, ein_ref, table_ref, turned_ref, mats_v_ref, mats_p_ref, *rest):
+    for lanes in lane_blocks(ein_ref.shape[1], width):
+        slots = slot_rows(index_ref, weight_ref, count_ref[0], lanes)
+        for i, (column, share) in enumerate(slots):
+            column_ref[i * PACK : (i + 1) * PACK, lanes] = column
+            share_ref[i * PACK : (i + 1) * PACK, lanes] = share
+        ein_ref[:, lanes] = matmul(flipped_ref[...], selection(slots, 0, owned))
+        if lanes.start < table_ref.shape[1]:
+            table = selection(slots[1:], owned, columns)
+            table_ref[:, lanes] = table
+            turned_ref[lanes, :] = table.T
+
+
+def element_kernel(width, pairs, owned, visc_ref, ein_ref, column_ref, share_ref, table_ref, turned_ref, mats_v_ref, mats_p_ref, *rest):
     n = len(pairs)
-    ghost_refs, out_ref, ret_refs, (ghost_all, total, back) = rest[:n], rest[n], rest[n + 1 : 2 * n + 1], rest[2 * n + 1 :]
-    ghost = ghost_refs[0].shape[0]
+    ghost_refs, out_ref, ret_refs, rest = rest[:n], rest[n], rest[n + 1 : 2 * n + 1], rest[2 * n + 1 :]
+    ghost_all, stacked_ref, late_ref, back = rest
+    ghost, channels = ghost_refs[0].shape
+    early, columns = table_ref.shape[1], table_ref.shape[0]
+    blocks = lane_blocks(ein_ref.shape[1], width)
     spots = []
     for (distance, parity), ghost_ref in zip(pairs, ghost_refs):
         sent = send_region(distance, parity)
@@ -148,34 +149,33 @@
         ghost_all[spot, :] = ghost_ref[...]
     flipped = transposed(ghost_all[...])
     both = jnp.concatenate([mats_v_ref[...].astype(jnp.float32).T, mats_p_ref[...].astype(jnp.float32).T], axis=1).astype(jnp.bfloat16)
-    total[...] = jnp.zeros_like(total)
-
-    def step(start):
-        lanes = pl.ds(start, width)
-        ein = ein_ref[:, lanes] + matmul(flipped, table_ref[:, lanes])
-        stacked = jnp.concatenate([ein * visc_ref[:, lanes], ein], axis=0).astype(jnp.bfloat16)
-        out = matmul(both, stacked).astype(jnp.bfloat16)
-        out_ref[:, lanes] = out
-        total[...] += matmul(out, turned_ref[lanes, :])
-
-    over_blocks(ein_ref.shape[1], width, unroll, step)
-    back[...] = total[...].T
+    for lanes in blocks:
+        if lanes.start < early:
+            table = table_ref[:, lanes]
+        else:
+            table = selection(load_rows(column_ref, share_ref, lanes, 1), owned, columns)
+            late_ref[pl.ds(lanes.start - early, width), :] = table.T
+        ein = ein_ref[:, lanes] + matmul(flipped, table)
+        stacked_ref[:channels, lanes] = (ein * visc_ref[:, lanes]).astype(jnp.bfloat16)
+        stacked_ref[channels:, lanes] = ein.astype(jnp.bfloat16)
+    for lanes in blocks:
+        out_ref[:, lanes] = matmul(both, stacked_ref[:, lanes]).astype(jnp.bfloat16)
+    total = matmul(out_ref[:, :early], turned_ref[...])
+    if early < ein_ref.shape[1]:
+        total = total + matmul(out_ref[:, early:], late_ref[...])
+    back[...] = total.T
     for spot, ret_ref in zip(spots, ret_refs):
         ret_ref[...] = back[spot, :].astype(jnp.bfloat16)
 
 
-def scatter_kernel(width, unroll, count_ref, index_ref, weight_ref, out_ref, names_ref, part_ref, *hit_refs):
+def scatter_kernel(width, column_ref, share_ref, out_ref, names_ref, part_ref, *rest):
+    hit_refs, turned_ref = rest[:-1], rest[-1]
     owned = part_ref.shape[0]
-    part_ref[...] = jnp.zeros_like(part_ref)
+    for lanes in lane_blocks(out_ref.shape[1], width):
+        turned_ref[lanes, :] = selection(load_rows(column_ref, share_ref, lanes, 0), 0, owned).T
+    part_ref[...] = matmul(out_ref[...], turned_ref[...]).T
     for m, hit_ref in enumerate(hit_refs):
         hit_ref[...] = one_hot(names_ref[pl.ds(m, 1), :], owned)
-
-    def step(start):
-        lanes = pl.ds(start, width)
-        slots = slot_rows(index_ref, weight_ref, count_ref, start, width)
-        part_ref[...] += matmul_nt(selection(slots, 0, owned, width), out_ref[:, lanes])
-
-    over_blocks(out_ref.shape[1], width, unroll, step)
 
 
 def finish_kernel(n, part_ref, *rest):
@@ -213,7 +213,8 @@
     regions, ghost = mirror_rows.shape[1:]
     elements = viscosity.shape[0]
     width = min(512, elements)
-    unroll = min(4, elements // width)
+    early = elements // 2
+    slots = slot_index.shape[1]
     pairs = matchings(regions)
     bf16, f32 = jnp.bfloat16, jnp.float32
     table_flops = 2 * elements * channels
@@ -243,45 +244,49 @@
     sent, (names, flipped, index, weight, visc, mats_v, mats_p) = outs[:regions], outs[regions:]
     got = [exchange(block, *pair) for block, pair in zip(sent, pairs)]
 
-    ein, table, turned = pl.pallas_call(
-        functools.partial(gather_kernel, width, unroll),
+    ein, column, share, table, turned = pl.pallas_call(
+        functools.partial(gather_kernel, width),
         out_shape=[
             jax.ShapeDtypeStruct((channels, elements), f32),
-            jax.ShapeDtypeStruct((regions * ghost, elements), bf16),
-            jax.ShapeDtypeStruct((elements, regions * ghost), bf16),
+            jax.ShapeDtypeStruct((PACK * slots, elements), jnp.int16),
+            jax.ShapeDtypeStruct((PACK * slots, elements), bf16),
+            jax.ShapeDtypeStruct((regions * ghost, early), bf16),
+            jax.ShapeDtypeStruct((early, regions * ghost), bf16),
         ],
         in_specs=[SMEM] + [VMEM] * 3,
-        out_specs=[VMEM] * 3,
+        out_specs=[VMEM] * 5,
         compiler_params=params(20),
         cost_estimate=cost(table_flops * owned * 8),
         name="gather_owned",
     )(cell_count, index, weight, flipped)
 
     out, *ret = pl.pallas_call(
-        functools.partial(element_kernel, width, unroll, pairs),
+        functools.partial(element_kernel, width, pairs, owned),
         out_shape=[jax.ShapeDtypeStruct((channels, elements), bf16)] + list_shape,
-        in_specs=[VMEM] * (6 + regions),
+        in_specs=[VMEM] * (8 + regions),
         out_specs=[VMEM] * (1 + regions),
         scratch_shapes=[
             pltpu.VMEM((regions * ghost, channels), bf16),
-            pltpu.VMEM((channels, regions * ghost), f32),
+            pltpu.VMEM((2 * channels, elements), bf16),
+            pltpu.VMEM((max(elements - early, PACK), regions * ghost), bf16),
             pltpu.VMEM((regions * ghost, channels), f32),
         ],
-        compiler_params=params(20),
+        compiler_params=params(24),
         cost_estimate=cost(table_flops * regions * ghost * 2),
         name="elements",
-    )(visc, ein, table, turned, mats_v, mats_p, *got)
+    )(visc, ein, column, share, table, turned, mats_v, mats_p, *got)
     back = [exchange(block, *pair) for block, pair in zip(ret, pairs)]
 
     part, *hits = pl.pallas_call(
-        functools.partial(scatter_kernel, width, unroll),
+        functools.partial(scatter_kernel, width),
         out_shape=[jax.ShapeDtypeStruct((owned, channels), f32)] + [jax.ShapeDtypeStruct((owned, ghost), bf16)] * regions,
-        in_specs=[SMEM] + [VMEM] * 4,
+        in_specs=[VMEM] * 4,
         out_specs=[VMEM] * (1 + regions),
-        compiler_params=params(20),
+        scratch_shapes=[pltpu.VMEM((elements, owned), bf16)],
+        compiler_params=params(24),
         cost_estimate=cost(table_flops * owned * 8),
         name="scatter_owned",
-    )(cell_count, index, weight, out, names)
+    )(column, share, out, names)
 
     return pl.pallas_call(
         functools.partial(finish_kernel, regions),

time: 32.2 us -> 29 us (0.901)
  the two profiles are of different devices: /device:TPU:17 before, /device:TPU:0 now
where the time goes in v1:
time: 29 us; the launch traced here: 28.7 us
  starting transfers between devices  17.6 us (61%)
  Pallas kernels  10.1 us (35%)
  between operations  0.76 us (3%)
  waiting for transfers between devices  0.35 us (1%)
    ppermute x8, starting transfers between devices, exchange(): return lax.ppermute(block, AXES, route)  17.6 us
    pallas_call x1, Pallas kernels, per_device(): pl.pallas_call(functools.partial(element_kernel, width, pairs, owned), ou...  3.03 us
    pallas_call x1, Pallas kernels, per_device(): pl.pallas_call(functools.partial(gather_kernel, width), out_shape=[jax.Sh...  2.5 us
    pallas_call x1, Pallas kernels, per_device(): pl.pallas_call(functools.partial(scatter_kernel, width), out_shape=[jax.S...  1.97 us
    pallas_call x1, Pallas kernels, per_device(): pl.pallas_call(functools.partial(select_kernel, pairs, len(loads)), out_s...  1.42 us
    pallas_call x1, Pallas kernels, per_device(): pl.pallas_call(functools.partial(finish_kernel, regions), out_shape=jax.S...  1.13 us
  transfers between devices with their start and end apart: 8, of which 1 were waited for; matrix products, arithmetic and copies ran while one was open for 0% of the time, Pallas kernels for 16%

profile of v1, /device:TPU:0, one launch (start us, length us, event | category | flops | bytes accessed | tf_op | source)
XLA Modules:
  0.0 28.7 jit_solution(16584879243512984456)
XLA Ops:
  0.0 1.4 %select.1 = (bf16[192,128]{1,0:T(8,128)(2,1)S(1)}, bf16[192,128]{1,0:T(8,128)(2,1)S(1)}, bf16[192,128]{1,0:T(8,128)(2,1)S(1)}, bf16[192,128]{1,0:T(8,128)(2,1)S(...) custom-call(s32[1,4,192]{2,1,0:T(4,128)} %mirror_hbm.1, ...), custom_call_target="tpu_custom_call" | custom-call | flops 100663296 | bytes 1048576 | tf_op jit(solution)/shard_map/select/pallas_call | solution.py:224
  1.4 0.7 %collective-permute-start = (bf16[192,128]{1,0:T(8,128)(2,1)S(1)}, bf16[192,128]{1,0:T(8,128)(2,1)S(1)}, u32[]{:S(2)}, u32[]{:S(2)}) collective-permute-start(bf16[192,128]{1,0:T(8,128)(2,1)S(1)} %get-tuple-element.42), channel_id=1, source_target_pairs={{2,4},{4,2},{3,5},{5,3},{6,8},{8,6},{7,9},{9,7},{10,12},{12,10},{1... | collective-permute-start | bytes 147464 | tf_op jit(solution)/shard_map/ppermute | solution.py:27
  2.1 0.7 %collective-permute-start.1 = (bf16[192,128]{1,0:T(8,128)(2,1)S(1)}, bf16[192,128]{1,0:T(8,128)(2,1)S(1)}, u32[]{:S(2)}, u32[]{:S(2)}) collective-permute-start(bf16[192,128]{1,0:T(8,128)(2,1)S(1)} %get-tuple-element.43), channel_id=1, source_target_pairs={{1,2},{2,1},{3,4},{4,3},{5,6},{6,5},{7,8},{8,7},{9,10},{10,9},{11,... | collective-permute-start | bytes 147464 | tf_op jit(solution)/shard_map/ppermute | solution.py:27
  2.8 7.0 %collective-permute-start.2 = (bf16[192,128]{1,0:T(8,128)(2,1)S(1)}, bf16[192,128]{1,0:T(8,128)(2,1)S(1)}, u32[]{:S(2)}, u32[]{:S(2)}) collective-permute-start(bf16[192,128]{1,0:T(8,128)(2,1)S(1)} %get-tuple-element.44), channel_id=1, source_target_pairs={{0,2},{2,0},{1,3},{3,1},{4,6},{6,4},{5,7},{7,5},{8,10},{10,8},{9,1... | collective-permute-start | bytes 147464 | tf_op jit(solution)/shard_map/ppermute | solution.py:27
  9.8 1.3 %collective-permute-start.3 = (bf16[192,128]{1,0:T(8,128)(2,1)S(1)}, bf16[192,128]{1,0:T(8,128)(2,1)S(1)}, u32[]{:S(2)}, u32[]{:S(2)}) collective-permute-start(bf16[192,128]{1,0:T(8,128)(2,1)S(1)} %get-tuple-element.45), channel_id=1, source_target_pairs={{0,1},{1,0},{2,3},{3,2},{4,5},{5,4},{6,7},{7,6},{8,9},{9,8},{10,11... | collective-permute-start | bytes 147464 | tf_op jit(solution)/shard_map/ppermute | solution.py:27
  11.7 2.5 %gather_owned.1 = (f32[128,4096]{1,0:T(8,128)S(1)}, s16[64,4096]{1,0:T(8,128)(2,1)S(1)}, bf16[64,4096]{1,0:T(8,128)(2,1)S(1)}, bf16[768,2048]{1,0:T(8,128)(2,1)S(1)}, bf16[2048,768]{1,0:T(8,128)(2,1)S(1)}) custom-call(s32[1]{0:T(128)S(6)} %copy.10.count_ref, s32[4,4096]{1,0:T(4,128)S(1)} %get-tuple-element.31.index_ref, ...), custom_call_target="tpu_custom_call" | custom-call | flops 4294967296 | bytes 1048576 | tf_op jit(solution)/shard_map/gather_owned/pallas_call | solution.py:247
  14.2 0.0 collective-permute-done.rest_0_
  14.2 0.0 collective-permute-done.1.rest_1_
  14.2 0.0 collective-permute-done.2.rest_2_
  14.2 0.0 collective-permute-done.3.rest_3_
  14.3 3.0 %elements.1 = (bf16[128,4096]{1,0:T(8,128)(2,1)S(1)}, bf16[192,128]{1,0:T(8,128)(2,1)S(1)}, bf16[192,128]{1,0:T(8,128)(2,1)S(1)}, bf16[192,128]{1,0:T(8,128)(2,1)S(1)}, bf16[192,128]{1,0:T(8,128)(2,1)S(1)}) custom-call(f32[1,4096]{1,0:T(1,128)S(1)} %get-tuple-element.36.visc_ref, f32[128,4096]{1,0:T(8,128)S(1)} %get-tuple-element.37.ein_ref, ...), custom_call_target="tpu_custom_call" | custom-call | flops 1610612736 | bytes 1048576 | tf_op jit(solution)/shard_map/elements/pallas_call | solution.py:263
  17.3 0.7 %collective-permute-start.4 = (bf16[192,128]{1,0:T(8,128)(2,1)S(1)}, bf16[192,128]{1,0:T(8,128)(2,1)S(1)}, u32[]{:S(2)}, u32[]{:S(2)}) collective-permute-start(bf16[192,128]{1,0:T(8,128)(2,1)S(1)} %get-tuple-element.53), channel_id=1, source_target_pairs={{2,4},{4,2},{3,5},{5,3},{6,8},{8,6},{7,9},{9,7},{10,12},{12,10},{1... | collective-permute-start | bytes 147464 | tf_op jit(solution)/shard_map/ppermute | solution.py:27
  18.0 0.7 %collective-permute-start.5 = (bf16[192,128]{1,0:T(8,128)(2,1)S(1)}, bf16[192,128]{1,0:T(8,128)(2,1)S(1)}, u32[]{:S(2)}, u32[]{:S(2)}) collective-permute-start(bf16[192,128]{1,0:T(8,128)(2,1)S(1)} %get-tuple-element.54), channel_id=1, source_target_pairs={{1,2},{2,1},{3,4},{4,3},{5,6},{6,5},{7,8},{8,7},{9,10},{10,9},{11,... | collective-permute-start | bytes 147464 | tf_op jit(solution)/shard_map/ppermute | solution.py:27
  18.6 6.4 %collective-permute-start.6 = (bf16[192,128]{1,0:T(8,128)(2,1)S(1)}, bf16[192,128]{1,0:T(8,128)(2,1)S(1)}, u32[]{:S(2)}, u32[]{:S(2)}) collective-permute-start(bf16[192,128]{1,0:T(8,128)(2,1)S(1)} %get-tuple-element.55), channel_id=1, source_target_pairs={{0,2},{2,0},{1,3},{3,1},{4,6},{6,4},{5,7},{7,5},{8,10},{10,8},{9,1... | collective-permute-start | bytes 147464 | tf_op jit(solution)/shard_map/ppermute | solution.py:27
  25.1 0.2 collective-permute-start.7
  25.3 2.0 %scatter_owned.1 = (f32[512,128]{1,0:T(8,128)S(1)}, bf16[512,192]{1,0:T(8,128)(2,1)S(1)}, bf16[512,192]{1,0:T(8,128)(2,1)S(1)}, bf16[512,192]{1,0:T(8,128)(2,1)S(1)}, bf16[512,192]{1,0:T(8,128)(2,1)S(1)}) custom-call(s16[64,4096]{1,0:T(8,128)(2,1)S(1)} %get-tuple-element.34.column_ref, bf16[64,4096]{1,0:T(8,128)(2,1)S(1)} %get-tuple-element.35.share_ref, ...), custom_call_target="tpu_custom_call" | custom-call | flops 4294967296 | bytes 1048576 | tf_op jit(solution)/shard_map/scatter_owned/pallas_call | solution.py:280
  27.3 0.0 collective-permute-done.4.rest_4_
  27.3 0.0 collective-permute-done.5.rest_5_
  27.3 0.3 %collective-permute-done.6.rest_6_ = bf16[192,128]{1,0:T(8,128)(2,1)S(1)} collective-permute-done((bf16[192,128]{1,0:T(8,128)(2,1)S(1)}, bf16[192,128]{1,0:T(8,128)(2,1)S(1)}, u32[]{:S(2)}, u32[]{:S(2)}) %collective-permute-start.6) | collective-permute-done | bytes 49184 | tf_op jit(solution)/shard_map/ppermute | solution.py:27
  27.6 0.0 collective-permute-done.7.rest_7_
  27.6 1.1 %finish.1 = f32[512,128]{1,0:T(8,128)} custom-call(f32[512,128]{1,0:T(8,128)S(1)} %get-tuple-element.48.part_ref, bf16[512,192]{1,0:T(8,128)(2,1)S(1)} %get-tuple-element.49.rest_0_, bf16[512,192]{1,0:T(8,128)(2,1)S(1)} %get-tuple-element.50.rest_1_, bf16[512,192]{1,0:T(8,128)(2,1)S(1)} %get-tuple-element.51.rest_2_, ...), custom_call_target="tpu_custom_call" | custom-call | flops 100663296 | bytes 1048576 | tf_op jit(solution)/shard_map/finish/pallas_call | solution.py:291
Async XLA Ops:
  1.4 12.8 %collective-permute-start = (bf16[192,128]{1,0:T(8,128)(2,1)S(1)}, bf16[192,128]{1,0:T(8,128)(2,1)S(1)}, u32[]{:S(2)}, u32[]{:S(2)}) collective-permute-start(bf16[192,128]{1,0:T(8,128)(2,1)S(1)} %get-tuple-element.42), channel_id=1, source_target_pairs={{2,4},{4,2},{3,5},{5,3},{6,8},{8,6},{7,9},{9,7},{10,12},{12,10},{1... | collective-permute-start | bytes 147464 | tf_op jit(solution)/shard_map/ppermute | solution.py:27
  2.1 12.1 %collective-permute-start.1 = (bf16[192,128]{1,0:T(8,128)(2,1)S(1)}, bf16[192,128]{1,0:T(8,128)(2,1)S(1)}, u32[]{:S(2)}, u32[]{:S(2)}) collective-permute-start(bf16[192,128]{1,0:T(8,128)(2,1)S(1)} %get-tuple-element.43), channel_id=1, source_target_pairs={{1,2},{2,1},{3,4},{4,3},{5,6},{6,5},{7,8},{8,7},{9,10},{10,9},{11,... | collective-permute-start | bytes 147464 | tf_op jit(solution)/shard_map/ppermute | solution.py:27
  2.8 11.5 %collective-permute-start.2 = (bf16[192,128]{1,0:T(8,128)(2,1)S(1)}, bf16[192,128]{1,0:T(8,128)(2,1)S(1)}, u32[]{:S(2)}, u32[]{:S(2)}) collective-permute-start(bf16[192,128]{1,0:T(8,128)(2,1)S(1)} %get-tuple-element.44), channel_id=1, source_target_pairs={{0,2},{2,0},{1,3},{3,1},{4,6},{6,4},{5,7},{7,5},{8,10},{10,8},{9,1... | collective-permute-start | bytes 147464 | tf_op jit(solution)/shard_map/ppermute | solution.py:27
  9.8 4.5 %collective-permute-start.3 = (bf16[192,128]{1,0:T(8,128)(2,1)S(1)}, bf16[192,128]{1,0:T(8,128)(2,1)S(1)}, u32[]{:S(2)}, u32[]{:S(2)}) collective-permute-start(bf16[192,128]{1,0:T(8,128)(2,1)S(1)} %get-tuple-element.45), channel_id=1, source_target_pairs={{0,1},{1,0},{2,3},{3,2},{4,5},{5,4},{6,7},{7,6},{8,9},{9,8},{10,11... | collective-permute-start | bytes 147464 | tf_op jit(solution)/shard_map/ppermute | solution.py:27
  17.3 10.0 %collective-permute-start.4 = (bf16[192,128]{1,0:T(8,128)(2,1)S(1)}, bf16[192,128]{1,0:T(8,128)(2,1)S(1)}, u32[]{:S(2)}, u32[]{:S(2)}) collective-permute-start(bf16[192,128]{1,0:T(8,128)(2,1)S(1)} %get-tuple-element.53), channel_id=1, source_target_pairs={{2,4},{4,2},{3,5},{5,3},{6,8},{8,6},{7,9},{9,7},{10,12},{12,10},{1... | collective-permute-start | bytes 147464 | tf_op jit(solution)/shard_map/ppermute | solution.py:27
  18.0 9.3 %collective-permute-start.5 = (bf16[192,128]{1,0:T(8,128)(2,1)S(1)}, bf16[192,128]{1,0:T(8,128)(2,1)S(1)}, u32[]{:S(2)}, u32[]{:S(2)}) collective-permute-start(bf16[192,128]{1,0:T(8,128)(2,1)S(1)} %get-tuple-element.54), channel_id=1, source_target_pairs={{1,2},{2,1},{3,4},{4,3},{5,6},{6,5},{7,8},{8,7},{9,10},{10,9},{11,... | collective-permute-start | bytes 147464 | tf_op jit(solution)/shard_map/ppermute | solution.py:27
  18.6 9.0 %collective-permute-start.6 = (bf16[192,128]{1,0:T(8,128)(2,1)S(1)}, bf16[192,128]{1,0:T(8,128)(2,1)S(1)}, u32[]{:S(2)}, u32[]{:S(2)}) collective-permute-start(bf16[192,128]{1,0:T(8,128)(2,1)S(1)} %get-tuple-element.55), channel_id=1, source_target_pairs={{0,2},{2,0},{1,3},{3,1},{4,6},{6,4},{5,7},{7,5},{8,10},{10,8},{9,1... | collective-permute-start | bytes 147464 | tf_op jit(solution)/shard_map/ppermute | solution.py:27
  25.1 2.5 %collective-permute-start.7 = (bf16[192,128]{1,0:T(8,128)(2,1)S(1)}, bf16[192,128]{1,0:T(8,128)(2,1)S(1)}, u32[]{:S(2)}, u32[]{:S(2)}) collective-permute-start(bf16[192,128]{1,0:T(8,128)(2,1)S(1)} %get-tuple-element.56), channel_id=1, source_target_pairs={{0,1},{1,0},{2,3},{3,2},{4,5},{5,4},{6,7},{7,6},{8,9},{9,8},{10,11... | collective-permute-start | bytes 147464 | tf_op jit(solution)/shard_map/ppermute | solution.py:27

commit v2 on v1

--- a/solution.py
+++ b/solution.py
@@ -15,22 +15,24 @@
 
 
 def matchings(region_count):
-    return [(reach + 1, parity) for parity in (1, 0) for reach in reversed(range(region_count // 2))]
+    reaches = range(1, region_count // 2 + 1)
+    return [(reach, 1) for reach in reaches] + [(reach, 0) for reach in reversed(reaches)]
 
 
 def exchange(block, distance, parity):
     total = lax.axis_size(AXES)
-    route = []
-    for d in range(total - distance):
-        if (d // distance) % 2 == parity:
-            route += [(d, d + distance), (d + distance, d)]
-    return lax.ppermute(block, AXES, route)
+    swaps = [(d, d + distance) for d in range(total - distance) if (d // distance) % 2 == parity]
+    left = sorted(set(range(total)) - {d for swap in swaps for d in swap})
+    swaps += list(zip(left[::2], left[1::2]))
+    return lax.ppermute(block, AXES, swaps + [(b, a) for a, b in swaps])
 
 
 def send_region(distance, parity):
-    me = lax.axis_index("curve") * lax.axis_size("seg") + lax.axis_index("seg")
-    up = (lax.div(me, distance) + parity) % 2
-    return 2 * (distance - 1) + up
+    seg = lax.axis_size("seg")
+    me = lax.axis_index("curve") * seg + lax.axis_index("seg")
+    down = (lax.div(me, distance) + parity) % 2
+    there = me + distance * (1 - 2 * down)
+    return 2 * (distance - 1) + down, (there >= 0) & (there < seg * lax.axis_size("curve"))
 
 
 def transposed(values):
@@ -71,8 +73,8 @@
     flipped_ref[...] = flipped
     lane = lax.broadcasted_iota(jnp.int32, (1, ghost), 1)
     for m, (distance, parity) in enumerate(pairs):
-        region = send_region(distance, parity)
-        names = jnp.where(lane < live_ref[0, region], mirror_ref[0, pl.ds(region, 1), :], -1)
+        region, there = send_region(distance, parity)
+        names = jnp.where(lane < jnp.where(there, live_ref[0, region], 0), mirror_ref[0, pl.ds(region, 1), :], -1)
         names_ref[pl.ds(m, 1), :] = names
         sent_refs[m][...] = matmul(flipped, one_hot(names, rows)).T.astype(jnp.bfloat16)
     for copy in later:
@@ -142,7 +144,7 @@
     blocks = lane_blocks(ein_ref.shape[1], width)
     spots = []
     for (distance, parity), ghost_ref in zip(pairs, ghost_refs):
-        sent = send_region(distance, parity)
+        sent, _ = send_region(distance, parity)
         got = 4 * (distance - 1) + 1 - sent
         spot = pl.ds(pl.multiple_of(got * ghost, PACK), ghost)
         spots.append(spot)

time: 29 us -> 23.7 us (0.82)
  starting transfers between devices: 17.6 us -> 11.2 us
  waiting for transfers between devices: 0.35 us -> 1.6 us
    ppermute x8, starting transfers between devices: 17.6 us -> 11.2 us  [exchange(): return lax.ppermute(block, AXES, swaps + [(b, a) for a, b in swaps])]
    ppermute x8, waiting for transfers between devices: 0.35 us -> 1.6 us  [exchange(): return lax.ppermute(block, AXES, swaps + [(b, a) for a, b in swaps])]
  transfers between devices with their start and end apart: 8 -> 8, of which waited for: 1 -> 3; matrix products, arithmetic and copies ran while one was open for 0% -> 0% of each run, Pallas kernels for 16% -> 19%
where the time goes in v2:
time: 23.7 us; the launch traced here: 23.5 us
  starting transfers between devices  11.2 us (47%)
  Pallas kernels  10.1 us (43%)
  waiting for transfers between devices  1.6 us (7%)
  between operations  0.7 us (3%)
    ppermute x8, starting transfers between devices, exchange(): return lax.ppermute(block, AXES, swaps + [(b, a) for a, b in swaps])  11.2 us
    pallas_call x1, Pallas kernels, per_device(): pl.pallas_call(functools.partial(element_kernel, width, pairs, owned), ou...  3.03 us
    pallas_call x1, Pallas kernels, per_device(): pl.pallas_call(functools.partial(gather_kernel, width), out_shape=[jax.Sh...  2.5 us
    pallas_call x1, Pallas kernels, per_device(): pl.pallas_call(functools.partial(scatter_kernel, width), out_shape=[jax.S...  1.98 us
    ppermute x8, waiting for transfers between devices, exchange(): return lax.ppermute(block, AXES, swaps + [(b, a) for a, b in swaps])  1.6 us
    pallas_call x1, Pallas kernels, per_device(): pl.pallas_call(functools.partial(select_kernel, pairs, len(loads)), out_s...  1.41 us
    pallas_call x1, Pallas kernels, per_device(): pl.pallas_call(functools.partial(finish_kernel, regions), out_shape=jax.S...  1.13 us
  transfers between devices with their start and end apart: 8, of which 3 were waited for; matrix products, arithmetic and copies ran while one was open for 0% of the time, Pallas kernels for 19%

profile of v2, /device:TPU:0, one launch (start us, length us, event | category | flops | bytes accessed | tf_op | source)
XLA Modules:
  0.0 23.5 jit_solution(2826592588489793961)
XLA Ops:
  0.0 1.4 %select.1 = (bf16[192,128]{1,0:T(8,128)(2,1)S(1)}, bf16[192,128]{1,0:T(8,128)(2,1)S(1)}, bf16[192,128]{1,0:T(8,128)(2,1)S(1)}, bf16[192,128]{1,0:T(8,128)(2,1)S(...) custom-call(s32[1,4,192]{2,1,0:T(4,128)} %mirror_hbm.1, ...), custom_call_target="tpu_custom_call" | custom-call | flops 100663296 | bytes 1048576 | tf_op jit(solution)/shard_map/select/pallas_call | solution.py:226
  1.4 6.5 %collective-permute-start = (bf16[192,128]{1,0:T(8,128)(2,1)S(1)}, bf16[192,128]{1,0:T(8,128)(2,1)S(1)}, u32[]{:S(2)}, u32[]{:S(2)}) collective-permute-start(bf16[192,128]{1,0:T(8,128)(2,1)S(1)} %get-tuple-element.42), channel_id=1, source_target_pairs={{1,2},{3,4},{5,6},{7,8},{9,10},{11,12},{13,14},{15,16},{17,18},{19... | collective-permute-start | bytes 147464 | tf_op jit(solution)/shard_map/ppermute | solution.py:27
  7.9 0.0 collective-permute-start.1
  7.9 0.0 collective-permute-start.2
  7.9 0.5 %collective-permute-start.3 = (bf16[192,128]{1,0:T(8,128)(2,1)S(1)}, bf16[192,128]{1,0:T(8,128)(2,1)S(1)}, u32[]{:S(2)}, u32[]{:S(2)}) collective-permute-start(bf16[192,128]{1,0:T(8,128)(2,1)S(1)} %get-tuple-element.45), channel_id=1, source_target_pairs={{0,1},{2,3},{4,5},{6,7},{8,9},{10,11},{12,13},{14,15},{16,17},{18,... | collective-permute-start | bytes 147464 | tf_op jit(solution)/shard_map/ppermute | solution.py:27
  9.1 2.5 %gather_owned.1 = (f32[128,4096]{1,0:T(8,128)S(1)}, s16[64,4096]{1,0:T(8,128)(2,1)S(1)}, bf16[64,4096]{1,0:T(8,128)(2,1)S(1)}, bf16[768,2048]{1,0:T(8,128)(2,1)S(1)}, bf16[2048,768]{1,0:T(8,128)(2,1)S(1)}) custom-call(s32[1]{0:T(128)S(6)} %copy.10.count_ref, s32[4,4096]{1,0:T(4,128)S(1)} %get-tuple-element.31.index_ref, ...), custom_call_target="tpu_custom_call" | custom-call | flops 4294967296 | bytes 1048576 | tf_op jit(solution)/shard_map/gather_owned/pallas_call | solution.py:249
  11.6 0.0 collective-permute-done.rest_0_
  11.6 0.0 collective-permute-done.1.rest_1_
  11.6 0.5 %collective-permute-done.2.rest_2_ = bf16[192,128]{1,0:T(8,128)(2,1)S(1)} collective-permute-done((bf16[192,128]{1,0:T(8,128)(2,1)S(1)}, bf16[192,128]{1,0:T(8,128)(2,1)S(1)}, u32[]{:S(2)}, u32[]{:S(2)}) %collective-permute-start.2) | collective-permute-done | bytes 49184 | tf_op jit(solution)/shard_map/ppermute | solution.py:27
  12.0 0.0 collective-permute-done.3.rest_3_
  12.0 3.0 %elements.1 = (bf16[128,4096]{1,0:T(8,128)(2,1)S(1)}, bf16[192,128]{1,0:T(8,128)(2,1)S(1)}, bf16[192,128]{1,0:T(8,128)(2,1)S(1)}, bf16[192,128]{1,0:T(8,128)(2,1)S(1)}, bf16[192,128]{1,0:T(8,128)(2,1)S(1)}) custom-call(f32[1,4096]{1,0:T(1,128)S(1)} %get-tuple-element.36.visc_ref, f32[128,4096]{1,0:T(8,128)S(1)} %get-tuple-element.37.ein_ref, ...), custom_call_target="tpu_custom_call" | custom-call | flops 1610612736 | bytes 1048576 | tf_op jit(solution)/shard_map/elements/pallas_call | solution.py:265
  15.1 3.0 %collective-permute-start.4 = (bf16[192,128]{1,0:T(8,128)(2,1)S(1)}, bf16[192,128]{1,0:T(8,128)(2,1)S(1)}, u32[]{:S(2)}, u32[]{:S(2)}) collective-permute-start(bf16[192,128]{1,0:T(8,128)(2,1)S(1)} %get-tuple-element.53), channel_id=1, source_target_pairs={{1,2},{3,4},{5,6},{7,8},{9,10},{11,12},{13,14},{15,16},{17,18},{19... | collective-permute-start | bytes 147464 | tf_op jit(solution)/shard_map/ppermute | solution.py:27
  18.1 0.0 collective-permute-start.5
  18.1 1.1 %collective-permute-start.6 = (bf16[192,128]{1,0:T(8,128)(2,1)S(1)}, bf16[192,128]{1,0:T(8,128)(2,1)S(1)}, u32[]{:S(2)}, u32[]{:S(2)}) collective-permute-start(bf16[192,128]{1,0:T(8,128)(2,1)S(1)} %get-tuple-element.55), channel_id=1, source_target_pairs={{0,2},{1,3},{4,6},{5,7},{8,10},{9,11},{12,14},{13,15},{16,18},{17,... | collective-permute-start | bytes 147464 | tf_op jit(solution)/shard_map/ppermute | solution.py:27
  19.3 0.0 collective-permute-start.7
  19.3 2.0 %scatter_owned.1 = (f32[512,128]{1,0:T(8,128)S(1)}, bf16[512,192]{1,0:T(8,128)(2,1)S(1)}, bf16[512,192]{1,0:T(8,128)(2,1)S(1)}, bf16[512,192]{1,0:T(8,128)(2,1)S(1)}, bf16[512,192]{1,0:T(8,128)(2,1)S(1)}) custom-call(s16[64,4096]{1,0:T(8,128)(2,1)S(1)} %get-tuple-element.34.column_ref, bf16[64,4096]{1,0:T(8,128)(2,1)S(1)} %get-tuple-element.35.share_ref, ...), custom_call_target="tpu_custom_call" | custom-call | flops 4294967296 | bytes 1048576 | tf_op jit(solution)/shard_map/scatter_owned/pallas_call | solution.py:282
  21.3 1.0 %collective-permute-done.4.rest_4_ = bf16[192,128]{1,0:T(8,128)(2,1)S(1)} collective-permute-done((bf16[192,128]{1,0:T(8,128)(2,1)S(1)}, bf16[192,128]{1,0:T(8,128)(2,1)S(1)}, u32[]{:S(2)}, u32[]{:S(2)}) %collective-permute-start.4) | collective-permute-done | bytes 49184 | tf_op jit(solution)/shard_map/ppermute | solution.py:27
  22.3 0.0 collective-permute-done.5.rest_5_
  22.3 0.1 collective-permute-done.6.rest_6_
  22.4 0.0 collective-permute-done.7.rest_7_
  22.4 1.1 %finish.1 = f32[512,128]{1,0:T(8,128)} custom-call(f32[512,128]{1,0:T(8,128)S(1)} %get-tuple-element.48.part_ref, bf16[512,192]{1,0:T(8,128)(2,1)S(1)} %get-tuple-element.49.rest_0_, bf16[512,192]{1,0:T(8,128)(2,1)S(1)} %get-tuple-element.50.rest_1_, bf16[512,192]{1,0:T(8,128)(2,1)S(1)} %get-tuple-element.51.rest_2_, ...), custom_call_target="tpu_custom_call" | custom-call | flops 100663296 | bytes 1048576 | tf_op jit(solution)/shard_map/finish/pallas_call | solution.py:293
Async XLA Ops:
  1.4 10.1 %collective-permute-start = (bf16[192,128]{1,0:T(8,128)(2,1)S(1)}, bf16[192,128]{1,0:T(8,128)(2,1)S(1)}, u32[]{:S(2)}, u32[]{:S(2)}) collective-permute-start(bf16[192,128]{1,0:T(8,128)(2,1)S(1)} %get-tuple-element.42), channel_id=1, source_target_pairs={{1,2},{3,4},{5,6},{7,8},{9,10},{11,12},{13,14},{15,16},{17,18},{19... | collective-permute-start | bytes 147464 | tf_op jit(solution)/shard_map/ppermute | solution.py:27
  7.9 3.7 %collective-permute-start.1 = (bf16[192,128]{1,0:T(8,128)(2,1)S(1)}, bf16[192,128]{1,0:T(8,128)(2,1)S(1)}, u32[]{:S(2)}, u32[]{:S(2)}) collective-permute-start(bf16[192,128]{1,0:T(8,128)(2,1)S(1)} %get-tuple-element.43), channel_id=1, source_target_pairs={{2,4},{3,5},{6,8},{7,9},{10,12},{11,13},{14,16},{15,17},{18,20},{1... | collective-permute-start | bytes 147464 | tf_op jit(solution)/shard_map/ppermute | solution.py:27
  7.9 4.2 %collective-permute-start.2 = (bf16[192,128]{1,0:T(8,128)(2,1)S(1)}, bf16[192,128]{1,0:T(8,128)(2,1)S(1)}, u32[]{:S(2)}, u32[]{:S(2)}) collective-permute-start(bf16[192,128]{1,0:T(8,128)(2,1)S(1)} %get-tuple-element.44), channel_id=1, source_target_pairs={{0,2},{1,3},{4,6},{5,7},{8,10},{9,11},{12,14},{13,15},{16,18},{17,... | collective-permute-start | bytes 147464 | tf_op jit(solution)/shard_map/ppermute | solution.py:27
  7.9 4.2 %collective-permute-start.3 = (bf16[192,128]{1,0:T(8,128)(2,1)S(1)}, bf16[192,128]{1,0:T(8,128)(2,1)S(1)}, u32[]{:S(2)}, u32[]{:S(2)}) collective-permute-start(bf16[192,128]{1,0:T(8,128)(2,1)S(1)} %get-tuple-element.45), channel_id=1, source_target_pairs={{0,1},{2,3},{4,5},{6,7},{8,9},{10,11},{12,13},{14,15},{16,17},{18,... | collective-permute-start | bytes 147464 | tf_op jit(solution)/shard_map/ppermute | solution.py:27
  15.1 7.2 %collective-permute-start.4 = (bf16[192,128]{1,0:T(8,128)(2,1)S(1)}, bf16[192,128]{1,0:T(8,128)(2,1)S(1)}, u32[]{:S(2)}, u32[]{:S(2)}) collective-permute-start(bf16[192,128]{1,0:T(8,128)(2,1)S(1)} %get-tuple-element.53), channel_id=1, source_target_pairs={{1,2},{3,4},{5,6},{7,8},{9,10},{11,12},{13,14},{15,16},{17,18},{19... | collective-permute-start | bytes 147464 | tf_op jit(solution)/shard_map/ppermute | solution.py:27
  18.1 4.1 %collective-permute-start.5 = (bf16[192,128]{1,0:T(8,128)(2,1)S(1)}, bf16[192,128]{1,0:T(8,128)(2,1)S(1)}, u32[]{:S(2)}, u32[]{:S(2)}) collective-permute-start(bf16[192,128]{1,0:T(8,128)(2,1)S(1)} %get-tuple-element.54), channel_id=1, source_target_pairs={{2,4},{3,5},{6,8},{7,9},{10,12},{11,13},{14,16},{15,17},{18,20},{1... | collective-permute-start | bytes 147464 | tf_op jit(solution)/shard_map/ppermute | solution.py:27
  18.1 4.3 %collective-permute-start.6 = (bf16[192,128]{1,0:T(8,128)(2,1)S(1)}, bf16[192,128]{1,0:T(8,128)(2,1)S(1)}, u32[]{:S(2)}, u32[]{:S(2)}) collective-permute-start(bf16[192,128]{1,0:T(8,128)(2,1)S(1)} %get-tuple-element.55), channel_id=1, source_target_pairs={{0,2},{1,3},{4,6},{5,7},{8,10},{9,11},{12,14},{13,15},{16,18},{17,... | collective-permute-start | bytes 147464 | tf_op jit(solution)/shard_map/ppermute | solution.py:27
  19.3 3.1 %collective-permute-start.7 = (bf16[192,128]{1,0:T(8,128)(2,1)S(1)}, bf16[192,128]{1,0:T(8,128)(2,1)S(1)}, u32[]{:S(2)}, u32[]{:S(2)}) collective-permute-start(bf16[192,128]{1,0:T(8,128)(2,1)S(1)} %get-tuple-element.56), channel_id=1, source_target_pairs={{0,1},{2,3},{4,5},{6,7},{8,9},{10,11},{12,13},{14,15},{16,17},{18,... | collective-permute-start | bytes 147464 | tf_op jit(solution)/shard_map/ppermute | solution.py:27

commit v3 on v2

--- a/solution.py
+++ b/solution.py
@@ -9,6 +9,7 @@
 
 AXES = ("curve", "seg")
 PACK = 16
+TILE = 256
 VMEM = pl.BlockSpec(memory_space=pltpu.VMEM)
 SMEM = pl.BlockSpec(memory_space=pltpu.SMEM)
 HBM = pl.BlockSpec(memory_space=pltpu.HBM)
@@ -117,31 +118,45 @@
     return jnp.concatenate(pieces, axis=0)
 
 
-def lane_blocks(total, width):
-    return [pl.ds(start, width) for start in range(0, total, width)]
-
-
-def gather_kernel(width, count_ref, index_ref, weight_ref, flipped_ref, ein_ref, column_ref, share_ref, table_ref, turned_ref):
+def spans(total, width):
+    return [pl.ds(start, min(width, total - start)) for start in range(0, total, width)]
+
+
+def by_load(count, total, work):
+    few = total // 4
+    if few % TILE:
+        return work(total)
+    pl.when(count <= few)(functools.partial(work, few))
+    pl.when(count > few)(functools.partial(work, total))
+
+
+def gather_kernel(width, early, count_ref, index_ref, weight_ref, flipped_ref, ein_ref, column_ref, share_ref, table_ref, turned_ref):
     owned, columns = flipped_ref.shape[1], table_ref.shape[0]
-    for lanes in lane_blocks(ein_ref.shape[1], width):
-        slots = slot_rows(index_ref, weight_ref, count_ref[0], lanes)
-        for i, (column, share) in enumerate(slots):
-            column_ref[i * PACK : (i + 1) * PACK, lanes] = column
-            share_ref[i * PACK : (i + 1) * PACK, lanes] = share
-        ein_ref[:, lanes] = matmul(flipped_ref[...], selection(slots, 0, owned))
-        if lanes.start < table_ref.shape[1]:
-            table = selection(slots[1:], owned, columns)
-            table_ref[:, lanes] = table
-            turned_ref[lanes, :] = table.T
-
-
-def element_kernel(width, pairs, owned, visc_ref, ein_ref, column_ref, share_ref, table_ref, turned_ref, mats_v_ref, mats_p_ref, *rest):
+
+    def work(total):
+        for lanes in spans(total, width):
+            slots = slot_rows(index_ref, weight_ref, count_ref[0], lanes)
+            for i, (column, share) in enumerate(slots):
+                column_ref[i * PACK : (i + 1) * PACK, lanes] = column
+                share_ref[i * PACK : (i + 1) * PACK, lanes] = share
+            ein_ref[:, lanes] = sum(matmul(flipped_ref[:, rows], selection(slots, rows.start, rows.size)) for rows in spans(owned, TILE))
+            if lanes.start < early:
+                for rows in spans(columns, TILE):
+                    table = selection(slots[1:], owned + rows.start, rows.size)
+                    table_ref[rows, lanes] = table
+                    turned_ref[lanes, rows] = table.T
+
+    by_load(count_ref[0], ein_ref.shape[1], work)
+
+
+def element_kernel(
+    width, early, pairs, owned, count_ref, visc_ref, ein_ref, column_ref, share_ref, table_ref, turned_ref, mats_v_ref, mats_p_ref, *rest
+):
     n = len(pairs)
     ghost_refs, out_ref, ret_refs, rest = rest[:n], rest[n], rest[n + 1 : 2 * n + 1], rest[2 * n + 1 :]
     ghost_all, stacked_ref, late_ref, back = rest
     ghost, channels = ghost_refs[0].shape
-    early, columns = table_ref.shape[1], table_ref.shape[0]
-    blocks = lane_blocks(ein_ref.shape[1], width)
+    columns = table_ref.shape[0]
     spots = []
     for (distance, parity), ghost_ref in zip(pairs, ghost_refs):
         sent, _ = send_region(distance, parity)
@@ -149,33 +164,48 @@
         spot = pl.ds(pl.multiple_of(got * ghost, PACK), ghost)
         spots.append(spot)
         ghost_all[spot, :] = ghost_ref[...]
-    flipped = transposed(ghost_all[...])
-    both = jnp.concatenate([mats_v_ref[...].astype(jnp.float32).T, mats_p_ref[...].astype(jnp.float32).T], axis=1).astype(jnp.bfloat16)
-    for lanes in blocks:
-        if lanes.start < early:
-            table = table_ref[:, lanes]
-        else:
-            table = selection(load_rows(column_ref, share_ref, lanes, 1), owned, columns)
-            late_ref[pl.ds(lanes.start - early, width), :] = table.T
-        ein = ein_ref[:, lanes] + matmul(flipped, table)
-        stacked_ref[:channels, lanes] = (ein * visc_ref[:, lanes]).astype(jnp.bfloat16)
-        stacked_ref[channels:, lanes] = ein.astype(jnp.bfloat16)
-    for lanes in blocks:
-        out_ref[:, lanes] = matmul(both, stacked_ref[:, lanes]).astype(jnp.bfloat16)
-    total = matmul(out_ref[:, :early], turned_ref[...])
-    if early < ein_ref.shape[1]:
-        total = total + matmul(out_ref[:, early:], late_ref[...])
-    back[...] = total.T
-    for spot, ret_ref in zip(spots, ret_refs):
-        ret_ref[...] = back[spot, :].astype(jnp.bfloat16)
-
-
-def scatter_kernel(width, column_ref, share_ref, out_ref, names_ref, part_ref, *rest):
+
+    def work(total):
+        flipped = transposed(ghost_all[...])
+        both = jnp.concatenate([mats_v_ref[...].astype(jnp.float32).T, mats_p_ref[...].astype(jnp.float32).T], axis=1).astype(jnp.bfloat16)
+        blocks = spans(total, width)
+        for lanes in blocks:
+            ein = ein_ref[:, lanes]
+            if lanes.start < early:
+                ein = ein + matmul(flipped, table_ref[:, lanes])
+            else:
+                slots = load_rows(column_ref, share_ref, lanes, 1)
+                for rows in spans(columns, TILE):
+                    table = selection(slots, owned + rows.start, rows.size)
+                    late_ref[pl.ds(lanes.start - early, width), rows] = table.T
+                    ein = ein + matmul(flipped[:, rows.start : rows.start + rows.size], table)
+            stacked_ref[:channels, lanes] = (ein * visc_ref[:, lanes]).astype(jnp.bfloat16)
+            stacked_ref[channels:, lanes] = ein.astype(jnp.bfloat16)
+        for lanes in blocks:
+            out_ref[:, lanes] = matmul(both, stacked_ref[:, lanes]).astype(jnp.bfloat16)
+        first = min(early, total)
+        summed = matmul(out_ref[:, :first], turned_ref[:first, :])
+        if total > early:
+            summed = summed + matmul(out_ref[:, early:total], late_ref[: total - early, :])
+        back[...] = summed.T
+        for spot, ret_ref in zip(spots, ret_refs):
+            ret_ref[...] = back[spot, :].astype(jnp.bfloat16)
+
+    by_load(count_ref[0], ein_ref.shape[1], work)
+
+
+def scatter_kernel(width, count_ref, column_ref, share_ref, out_ref, names_ref, part_ref, *rest):
     hit_refs, turned_ref = rest[:-1], rest[-1]
     owned = part_ref.shape[0]
-    for lanes in lane_blocks(out_ref.shape[1], width):
-        turned_ref[lanes, :] = selection(load_rows(column_ref, share_ref, lanes, 0), 0, owned).T
-    part_ref[...] = matmul(out_ref[...], turned_ref[...]).T
+
+    def work(total):
+        for lanes in spans(total, width):
+            slots = load_rows(column_ref, share_ref, lanes, 0)
+            for rows in spans(owned, TILE):
+                turned_ref[lanes, rows] = selection(slots, rows.start, rows.size).T
+        part_ref[...] = matmul(out_ref[:, :total], turned_ref[:total, :]).T
+
+    by_load(count_ref[0], out_ref.shape[1], work)
     for m, hit_ref in enumerate(hit_refs):
         hit_ref[...] = one_hot(names_ref[pl.ds(m, 1), :], owned)
 
@@ -214,7 +244,7 @@
     owned, channels = solution.shape
     regions, ghost = mirror_rows.shape[1:]
     elements = viscosity.shape[0]
-    width = min(512, elements)
+    width = min(TILE, elements)
     early = elements // 2
     slots = slot_index.shape[1]
     pairs = matchings(regions)
@@ -247,7 +277,7 @@
     got = [exchange(block, *pair) for block, pair in zip(sent, pairs)]
 
     ein, column, share, table, turned = pl.pallas_call(
-        functools.partial(gather_kernel, width),
+        functools.partial(gather_kernel, width, early),
         out_shape=[
             jax.ShapeDtypeStruct((channels, elements), f32),
             jax.ShapeDtypeStruct((PACK * slots, elements), jnp.int16),
@@ -263,9 +293,9 @@
     )(cell_count, index, weight, flipped)
 
     out, *ret = pl.pallas_call(
-        functools.partial(element_kernel, width, pairs, owned),
+        functools.partial(element_kernel, width, early, pairs, owned),
         out_shape=[jax.ShapeDtypeStruct((channels, elements), bf16)] + list_shape,
-        in_specs=[VMEM] * (8 + regions),
+        in_specs=[SMEM] + [VMEM] * (8 + regions),
         out_specs=[VMEM] * (1 + regions),
         scratch_shapes=[
             pltpu.VMEM((regions * ghost, channels), bf16),
@@ -276,19 +306,19 @@
         compiler_params=params(24),
         cost_estimate=cost(table_flops * regions * ghost * 2),
         name="elements",
-    )(visc, ein, column, share, table, turned, mats_v, mats_p, *got)
+    )(cell_count, visc, ein, column, share, table, turned, mats_v, mats_p, *got)
     back = [exchange(block, *pair) for block, pair in zip(ret, pairs)]
 
     part, *hits = pl.pallas_call(
         functools.partial(scatter_kernel, width),
         out_shape=[jax.ShapeDtypeStruct((owned, channels), f32)] + [jax.ShapeDtypeStruct((owned, ghost), bf16)] * regions,
-        in_specs=[VMEM] * 4,
+        in_specs=[SMEM] + [VMEM] * 4,
         out_specs=[VMEM] * (1 + regions),
         scratch_shapes=[pltpu.VMEM((elements, owned), bf16)],
         compiler_params=params(24),
         cost_estimate=cost(table_flops * owned * 8),
         name="scatter_owned",
-    )(column, share, out, names)
+    )(cell_count, column, share, out, names)
 
     return pl.pallas_call(
         functools.partial(finish_kernel, regions),

time: 23.7 us -> 23.2 us (0.979)
  Pallas kernels: 10.1 us -> 5.41 us
  waiting for transfers between devices: 1.6 us -> 3.76 us
  starting transfers between devices: 11.2 us -> 13.2 us
    pallas_call x2, Pallas kernels: 5.53 us -> 2 us  [the longest x1 1.07 us: per_device(): pl.pallas_call(functools.partial(element_kernel, width, early, pairs, own...]
    ppermute x8, waiting for transfers between devices: 1.6 us -> 3.76 us  [exchange(): return lax.ppermute(block, AXES, swaps + [(b, a) for a, b in swaps])]
    ppermute x8, starting transfers between devices: 11.2 us -> 13.2 us  [exchange(): return lax.ppermute(block, AXES, swaps + [(b, a) for a, b in swaps])]
    pallas_call x1, Pallas kernels: 1.98 us -> 0.86 us  [per_device(): pl.pallas_call(functools.partial(scatter_kernel, width), out_shape=[jax.S...]
  transfers between devices with their start and end apart: 8 -> 8, of which waited for: 3 -> 3; matrix products, arithmetic and copies ran while one was open for 0% -> 0% of each run, Pallas kernels for 19% -> 8%
where the time goes in v3:
time: 23.2 us; the launch traced here: 23 us
  starting transfers between devices  13.2 us (57%)
  Pallas kernels  5.41 us (23%)
  waiting for transfers between devices  3.76 us (16%)
  between operations  0.71 us (3%)
    ppermute x8, starting transfers between devices, exchange(): return lax.ppermute(block, AXES, swaps + [(b, a) for a, b in swaps])  13.2 us
    ppermute x8, waiting for transfers between devices, exchange(): return lax.ppermute(block, AXES, swaps + [(b, a) for a, b in swaps])  3.76 us
    pallas_call x1, Pallas kernels, per_device(): pl.pallas_call(functools.partial(select_kernel, pairs, len(loads)), out_s...  1.41 us
    pallas_call x1, Pallas kernels, per_device(): pl.pallas_call(functools.partial(finish_kernel, regions), out_shape=jax.S...  1.13 us
    pallas_call x1, Pallas kernels, per_device(): pl.pallas_call(functools.partial(element_kernel, width, early, pairs, own...  1.07 us
    pallas_call x1, Pallas kernels, per_device(): pl.pallas_call(functools.partial(gather_kernel, width, early), out_shape=...  0.93 us
    pallas_call x1, Pallas kernels, per_device(): pl.pallas_call(functools.partial(scatter_kernel, width), out_shape=[jax.S...  0.86 us
  transfers between devices with their start and end apart: 8, of which 3 were waited for; matrix products, arithmetic and copies ran while one was open for 0% of the time, Pallas kernels for 8%

profile of v3, /device:TPU:0, one launch (start us, length us, event | category | flops | bytes accessed | tf_op | source)
XLA Modules:
  0.0 23.0 jit_solution(10467418578974680567)
XLA Ops:
  0.0 1.4 %select.1 = (bf16[192,128]{1,0:T(8,128)(2,1)S(1)}, bf16[192,128]{1,0:T(8,128)(2,1)S(1)}, bf16[192,128]{1,0:T(8,128)(2,1)S(1)}, bf16[192,128]{1,0:T(8,128)(2,1)S(...) custom-call(s32[1,4,192]{2,1,0:T(4,128)} %mirror_hbm.1, ...), custom_call_target="tpu_custom_call" | custom-call | flops 100663296 | bytes 1048576 | tf_op jit(solution)/shard_map/select/pallas_call | solution.py:256
  1.4 6.5 %collective-permute-start = (bf16[192,128]{1,0:T(8,128)(2,1)S(1)}, bf16[192,128]{1,0:T(8,128)(2,1)S(1)}, u32[]{:S(2)}, u32[]{:S(2)}) collective-permute-start(bf16[192,128]{1,0:T(8,128)(2,1)S(1)} %get-tuple-element.42), channel_id=1, source_target_pairs={{1,2},{3,4},{5,6},{7,8},{9,10},{11,12},{13,14},{15,16},{17,18},{19... | collective-permute-start | bytes 147464 | tf_op jit(solution)/shard_map/ppermute | solution.py:28
  7.9 0.0 collective-permute-start.1
  7.9 0.0 collective-permute-start.2
  7.9 0.5 %collective-permute-start.3 = (bf16[192,128]{1,0:T(8,128)(2,1)S(1)}, bf16[192,128]{1,0:T(8,128)(2,1)S(1)}, u32[]{:S(2)}, u32[]{:S(2)}) collective-permute-start(bf16[192,128]{1,0:T(8,128)(2,1)S(1)} %get-tuple-element.45), channel_id=1, source_target_pairs={{0,1},{2,3},{4,5},{6,7},{8,9},{10,11},{12,13},{14,15},{16,17},{18,... | collective-permute-start | bytes 147464 | tf_op jit(solution)/shard_map/ppermute | solution.py:28
  9.1 0.9 %gather_owned.1 = (f32[128,4096]{1,0:T(8,128)S(1)}, s16[64,4096]{1,0:T(8,128)(2,1)S(1)}, bf16[64,4096]{1,0:T(8,128)(2,1)S(1)}, bf16[768,2048]{1,0:T(8,128)(2,1)S(1)}, bf16[2048,768]{1,0:T(8,128)(2,1)S(1)}) custom-call(s32[1]{0:T(128)S(6)} %copy.10.count_ref, s32[4,4096]{1,0:T(4,128)S(1)} %get-tuple-element.31.index_ref, ...), custom_call_target="tpu_custom_call" | custom-call | flops 4294967296 | bytes 1048576 | tf_op jit(solution)/shard_map/gather_owned/pallas_call | solution.py:279
  10.0 0.0 collective-permute-done.rest_0_
  10.0 0.0 collective-permute-done.1.rest_1_
  10.0 2.0 %collective-permute-done.2.rest_2_ = bf16[192,128]{1,0:T(8,128)(2,1)S(1)} collective-permute-done((bf16[192,128]{1,0:T(8,128)(2,1)S(1)}, bf16[192,128]{1,0:T(8,128)(2,1)S(1)}, u32[]{:S(2)}, u32[]{:S(2)}) %collective-permute-start.2) | collective-permute-done | bytes 49184 | tf_op jit(solution)/shard_map/ppermute | solution.py:28
  12.0 0.0 collective-permute-done.3.rest_3_
  12.0 1.1 %elements.1 = (bf16[128,4096]{1,0:T(8,128)(2,1)S(1)}, bf16[192,128]{1,0:T(8,128)(2,1)S(1)}, bf16[192,128]{1,0:T(8,128)(2,1)S(1)}, bf16[192,128]{1,0:T(8,128)(2,1)S(1)}, bf16[192,128]{1,0:T(8,128)(2,1)S(1)}) custom-call(s32[1]{0:T(128)S(6)} %copy.10.count_ref, f32[1,4096]{1,0:T(1,128)S(1)} %get-tuple-element.36.visc_ref, ...), custom_call_target="tpu_custom_call" | custom-call | flops 1610612736 | bytes 1048576 | tf_op jit(solution)/shard_map/elements/pallas_call | solution.py:295
  13.1 3.0 %collective-permute-start.4 = (bf16[192,128]{1,0:T(8,128)(2,1)S(1)}, bf16[192,128]{1,0:T(8,128)(2,1)S(1)}, u32[]{:S(2)}, u32[]{:S(2)}) collective-permute-start(bf16[192,128]{1,0:T(8,128)(2,1)S(1)} %get-tuple-element.53), channel_id=1, source_target_pairs={{1,2},{3,4},{5,6},{7,8},{9,10},{11,12},{13,14},{15,16},{17,18},{19... | collective-permute-start | bytes 147464 | tf_op jit(solution)/shard_map/ppermute | solution.py:28
  16.2 0.0 collective-permute-start.5
  16.2 3.1 %collective-permute-start.6 = (bf16[192,128]{1,0:T(8,128)(2,1)S(1)}, bf16[192,128]{1,0:T(8,128)(2,1)S(1)}, u32[]{:S(2)}, u32[]{:S(2)}) collective-permute-start(bf16[192,128]{1,0:T(8,128)(2,1)S(1)} %get-tuple-element.55), channel_id=1, source_target_pairs={{0,2},{1,3},{4,6},{5,7},{8,10},{9,11},{12,14},{13,15},{16,18},{17,... | collective-permute-start | bytes 147464 | tf_op jit(solution)/shard_map/ppermute | solution.py:28
  19.3 0.0 collective-permute-start.7
  19.3 0.9 %scatter_owned.1 = (f32[512,128]{1,0:T(8,128)S(1)}, bf16[512,192]{1,0:T(8,128)(2,1)S(1)}, bf16[512,192]{1,0:T(8,128)(2,1)S(1)}, bf16[512,192]{1,0:T(8,128)(2,1)S(1)}, bf16[512,192]{1,0:T(8,128)(2,1)S(1)}) custom-call(s32[1]{0:T(128)S(6)} %copy.10.count_ref, s16[64,4096]{1,0:T(8,128)(2,1)S(1)} %get-tuple-element.34.column_ref, ...), custom_call_target="tpu_custom_call" | custom-call | flops 4294967296 | bytes 1048576 | tf_op jit(solution)/shard_map/scatter_owned/pallas_call | solution.py:312
  20.2 0.1 collective-permute-done.4.rest_4_
  20.3 0.0 collective-permute-done.5.rest_5_
  20.3 1.6 %collective-permute-done.6.rest_6_ = bf16[192,128]{1,0:T(8,128)(2,1)S(1)} collective-permute-done((bf16[192,128]{1,0:T(8,128)(2,1)S(1)}, bf16[192,128]{1,0:T(8,128)(2,1)S(1)}, u32[]{:S(2)}, u32[]{:S(2)}) %collective-permute-start.6) | collective-permute-done | bytes 49184 | tf_op jit(solution)/shard_map/ppermute | solution.py:28
  21.9 0.0 collective-permute-done.7.rest_7_
  21.9 1.1 %finish.1 = f32[512,128]{1,0:T(8,128)} custom-call(f32[512,128]{1,0:T(8,128)S(1)} %get-tuple-element.48.part_ref, bf16[512,192]{1,0:T(8,128)(2,1)S(1)} %get-tuple-element.49.rest_0_, bf16[512,192]{1,0:T(8,128)(2,1)S(1)} %get-tuple-element.50.rest_1_, bf16[512,192]{1,0:T(8,128)(2,1)S(1)} %get-tuple-element.51.rest_2_, ...), custom_call_target="tpu_custom_call" | custom-call | flops 100663296 | bytes 1048576 | tf_op jit(solution)/shard_map/finish/pallas_call | solution.py:323
Async XLA Ops:
  1.4 8.6 %collective-permute-start = (bf16[192,128]{1,0:T(8,128)(2,1)S(1)}, bf16[192,128]{1,0:T(8,128)(2,1)S(1)}, u32[]{:S(2)}, u32[]{:S(2)}) collective-permute-start(bf16[192,128]{1,0:T(8,128)(2,1)S(1)} %get-tuple-element.42), channel_id=1, source_target_pairs={{1,2},{3,4},{5,6},{7,8},{9,10},{11,12},{13,14},{15,16},{17,18},{19... | collective-permute-start | bytes 147464 | tf_op jit(solution)/shard_map/ppermute | solution.py:28
  7.9 2.1 %collective-permute-start.1 = (bf16[192,128]{1,0:T(8,128)(2,1)S(1)}, bf16[192,128]{1,0:T(8,128)(2,1)S(1)}, u32[]{:S(2)}, u32[]{:S(2)}) collective-permute-start(bf16[192,128]{1,0:T(8,128)(2,1)S(1)} %get-tuple-element.43), channel_id=1, source_target_pairs={{2,4},{3,5},{6,8},{7,9},{10,12},{11,13},{14,16},{15,17},{18,20},{1... | collective-permute-start | bytes 147464 | tf_op jit(solution)/shard_map/ppermute | solution.py:28
  7.9 4.2 %collective-permute-start.2 = (bf16[192,128]{1,0:T(8,128)(2,1)S(1)}, bf16[192,128]{1,0:T(8,128)(2,1)S(1)}, u32[]{:S(2)}, u32[]{:S(2)}) collective-permute-start(bf16[192,128]{1,0:T(8,128)(2,1)S(1)} %get-tuple-element.44), channel_id=1, source_target_pairs={{0,2},{1,3},{4,6},{5,7},{8,10},{9,11},{12,14},{13,15},{16,18},{17,... | collective-permute-start | bytes 147464 | tf_op jit(solution)/shard_map/ppermute | solution.py:28
  7.9 4.2 %collective-permute-start.3 = (bf16[192,128]{1,0:T(8,128)(2,1)S(1)}, bf16[192,128]{1,0:T(8,128)(2,1)S(1)}, u32[]{:S(2)}, u32[]{:S(2)}) collective-permute-start(bf16[192,128]{1,0:T(8,128)(2,1)S(1)} %get-tuple-element.45), channel_id=1, source_target_pairs={{0,1},{2,3},{4,5},{6,7},{8,9},{10,11},{12,13},{14,15},{16,17},{18,... | collective-permute-start | bytes 147464 | tf_op jit(solution)/shard_map/ppermute | solution.py:28
  13.1 7.2 %collective-permute-start.4 = (bf16[192,128]{1,0:T(8,128)(2,1)S(1)}, bf16[192,128]{1,0:T(8,128)(2,1)S(1)}, u32[]{:S(2)}, u32[]{:S(2)}) collective-permute-start(bf16[192,128]{1,0:T(8,128)(2,1)S(1)} %get-tuple-element.53), channel_id=1, source_target_pairs={{1,2},{3,4},{5,6},{7,8},{9,10},{11,12},{13,14},{15,16},{17,18},{19... | collective-permute-start | bytes 147464 | tf_op jit(solution)/shard_map/ppermute | solution.py:28
  16.2 4.2 %collective-permute-start.5 = (bf16[192,128]{1,0:T(8,128)(2,1)S(1)}, bf16[192,128]{1,0:T(8,128)(2,1)S(1)}, u32[]{:S(2)}, u32[]{:S(2)}) collective-permute-start(bf16[192,128]{1,0:T(8,128)(2,1)S(1)} %get-tuple-element.54), channel_id=1, source_target_pairs={{2,4},{3,5},{6,8},{7,9},{10,12},{11,13},{14,16},{15,17},{18,20},{1... | collective-permute-start | bytes 147464 | tf_op jit(solution)/shard_map/ppermute | solution.py:28
  16.2 5.7 %collective-permute-start.6 = (bf16[192,128]{1,0:T(8,128)(2,1)S(1)}, bf16[192,128]{1,0:T(8,128)(2,1)S(1)}, u32[]{:S(2)}, u32[]{:S(2)}) collective-permute-start(bf16[192,128]{1,0:T(8,128)(2,1)S(1)} %get-tuple-element.55), channel_id=1, source_target_pairs={{0,2},{1,3},{4,6},{5,7},{8,10},{9,11},{12,14},{13,15},{16,18},{17,... | collective-permute-start | bytes 147464 | tf_op jit(solution)/shard_map/ppermute | solution.py:28
  19.3 2.6 %collective-permute-start.7 = (bf16[192,128]{1,0:T(8,128)(2,1)S(1)}, bf16[192,128]{1,0:T(8,128)(2,1)S(1)}, u32[]{:S(2)}, u32[]{:S(2)}) collective-permute-start(bf16[192,128]{1,0:T(8,128)(2,1)S(1)} %get-tuple-element.56), channel_id=1, source_target_pairs={{0,1},{2,3},{4,5},{6,7},{8,9},{10,11},{12,13},{14,15},{16,17},{18,... | collective-permute-start | bytes 147464 | tf_op jit(solution)/shard_map/ppermute | solution.py:28

commit v4 on v3

--- a/solution.py
+++ b/solution.py
@@ -7,6 +7,7 @@
 from jax.experimental.pallas import tpu as pltpu
 from jax.sharding import PartitionSpec as P
 
+
 AXES = ("curve", "seg")
 PACK = 16
 TILE = 256
@@ -20,20 +21,55 @@
     return [(reach, 1) for reach in reaches] + [(reach, 0) for reach in reversed(reaches)]
 
 
-def exchange(block, distance, parity):
-    total = lax.axis_size(AXES)
-    swaps = [(d, d + distance) for d in range(total - distance) if (d // distance) % 2 == parity]
-    left = sorted(set(range(total)) - {d for swap in swaps for d in swap})
-    swaps += list(zip(left[::2], left[1::2]))
-    return lax.ppermute(block, AXES, swaps + [(b, a) for a, b in swaps])
+def both_ways(swaps):
+    return swaps + [(b, a) for a, b in swaps]
+
+
+def ring(*devices):
+    return list(zip(devices, devices[1:] + devices[:1]))
+
+
+def exchange(blocks, pairs):
+    n = lax.axis_size(AXES)
+    routes = []
+    for distance, parity in pairs:
+        swaps = [(d, d + distance) for d in range(n - distance) if (d // distance) % 2 == parity]
+        left = sorted(set(range(n)) - {d for swap in swaps for d in swap})
+        if left == [0, n - 1]:
+            detour = ring(2, 1, 0, 3) + both_ways([(d, d + 1) for d in range(4, n - 4, 2)]) + ring(n - 3, n - 2, n - 1, n - 4)
+            routes.append(ring(0, 1, 2) + both_ways(swaps[1:-1]) + ring(n - 1, n - 2, n - 3))
+            source = len(routes) - 1
+        else:
+            routes.append(both_ways(swaps + list(zip(left[::2], left[1::2]))))
+    routes.append(detour)
+    got = []
+    for block, route in zip([*blocks, blocks[source]], routes):
+        got.append(lax.ppermute(block, AXES, route))
+    return got
+
+
+def position():
+    return lax.axis_index("curve") * lax.axis_size("seg") + lax.axis_index("seg"), lax.axis_size("curve") * lax.axis_size("seg")
+
+
+def received(pairs, refs):
+    me, total = position()
+    detoured = (me == 1) | (me == total - 2)
+    out = []
+    for (distance, parity), ref in zip(pairs, refs):
+        value = ref[...]
+        if (distance, parity) == (1, 1):
+            value = jnp.where(detoured, refs[-1][...], value)
+            value = jnp.where((me == 0) | (me == total - 1), jnp.zeros_like(value), value)
+        out.append(value)
+    return out
 
 
 def send_region(distance, parity):
-    seg = lax.axis_size("seg")
-    me = lax.axis_index("curve") * seg + lax.axis_index("seg")
+    me, total = position()
     down = (lax.div(me, distance) + parity) % 2
     there = me + distance * (1 - 2 * down)
-    return 2 * (distance - 1) + down, (there >= 0) & (there < seg * lax.axis_size("curve"))
+    return 2 * (distance - 1) + down, (there >= 0) & (there < total)
 
 
 def transposed(values):
@@ -42,10 +78,6 @@
 
 def matmul(a, b):
     return jnp.dot(a, b, preferred_element_type=jnp.float32)
-
-
-def matmul_nt(a, b):
-    return lax.dot_general(a, b, (((1,), (1,)), ((), ())), preferred_element_type=jnp.float32)
 
 
 def one_hot(names, rows):
@@ -153,17 +185,17 @@
     width, early, pairs, owned, count_ref, visc_ref, ein_ref, column_ref, share_ref, table_ref, turned_ref, mats_v_ref, mats_p_ref, *rest
 ):
     n = len(pairs)
-    ghost_refs, out_ref, ret_refs, rest = rest[:n], rest[n], rest[n + 1 : 2 * n + 1], rest[2 * n + 1 :]
+    ghost_refs, out_ref, ret_refs, rest = rest[: n + 1], rest[n + 1], rest[n + 2 : 2 * n + 2], rest[2 * n + 2 :]
     ghost_all, stacked_ref, late_ref, back = rest
     ghost, channels = ghost_refs[0].shape
     columns = table_ref.shape[0]
     spots = []
-    for (distance, parity), ghost_ref in zip(pairs, ghost_refs):
+    for (distance, parity), arrived in zip(pairs, received(pairs, ghost_refs)):
         sent, _ = send_region(distance, parity)
         got = 4 * (distance - 1) + 1 - sent
         spot = pl.ds(pl.multiple_of(got * ghost, PACK), ghost)
         spots.append(spot)
-        ghost_all[spot, :] = ghost_ref[...]
+        ghost_all[spot, :] = arrived
 
     def work(total):
         flipped = transposed(ghost_all[...])
@@ -210,11 +242,12 @@
         hit_ref[...] = one_hot(names_ref[pl.ds(m, 1), :], owned)
 
 
-def finish_kernel(n, part_ref, *rest):
-    hit_refs, back_refs, res_ref = rest[:n], rest[n : 2 * n], rest[2 * n]
+def finish_kernel(pairs, part_ref, *rest):
+    n = len(pairs)
+    hit_refs, back_refs, res_ref = rest[:n], rest[n : 2 * n + 1], rest[2 * n + 1]
     total = part_ref[...]
-    for hit_ref, back_ref in zip(hit_refs, back_refs):
-        total = total + matmul(hit_ref[...], back_ref[...])
+    for hit_ref, arrived in zip(hit_refs, received(pairs, back_refs)):
+        total = total + matmul(hit_ref[...], arrived)
     res_ref[...] = total
 
 
@@ -274,7 +307,7 @@
         name="select",
     )(*[pltpu.with_memory_space_constraint(a, pltpu.HBM) for a in (mirror_rows, ghost_live, solution, *loads)])
     sent, (names, flipped, index, weight, visc, mats_v, mats_p) = outs[:regions], outs[regions:]
-    got = [exchange(block, *pair) for block, pair in zip(sent, pairs)]
+    got = exchange(sent, pairs)
 
     ein, column, share, table, turned = pl.pallas_call(
         functools.partial(gather_kernel, width, early),
@@ -295,7 +328,7 @@
     out, *ret = pl.pallas_call(
         functools.partial(element_kernel, width, early, pairs, owned),
         out_shape=[jax.ShapeDtypeStruct((channels, elements), bf16)] + list_shape,
-        in_specs=[SMEM] + [VMEM] * (8 + regions),
+        in_specs=[SMEM] + [VMEM] * (9 + regions),
         out_specs=[VMEM] * (1 + regions),
         scratch_shapes=[
             pltpu.VMEM((regions * ghost, channels), bf16),
@@ -307,7 +340,7 @@
         cost_estimate=cost(table_flops * regions * ghost * 2),
         name="elements",
     )(cell_count, visc, ein, column, share, table, turned, mats_v, mats_p, *got)
-    back = [exchange(block, *pair) for block, pair in zip(ret, pairs)]
+    back = exchange(ret, pairs)
 
     part, *hits = pl.pallas_call(
         functools.partial(scatter_kernel, width),
@@ -321,9 +354,9 @@
     )(cell_count, column, share, out, names)
 
     return pl.pallas_call(
-        functools.partial(finish_kernel, regions),
+        functools.partial(finish_kernel, pairs),
         out_shape=jax.ShapeDtypeStruct((owned, channels), f32),
-        in_specs=[VMEM] * (1 + 2 * regions),
+        in_specs=[VMEM] * (2 + 2 * regions),
         out_specs=VMEM,
         compiler_params=params(16),
         cost_estimate=cost(2 * owned * channels * regions * ghost),

time: 23.2 us -> 23.1 us (level)
  Pallas kernels: 5.41 us -> 10.2 us
  starting transfers between devices: 13.2 us -> 10.5 us
  waiting for transfers between devices: 3.76 us -> 1.51 us
    ppermute x8 -> x10, starting transfers between devices: 13.2 us -> 10.5 us  [exchange(): got.append(lax.ppermute(block, AXES, route))]
    ppermute x8 -> x10, waiting for transfers between devices: 3.76 us -> 1.51 us  [exchange(): got.append(lax.ppermute(block, AXES, route))]
    pallas_call x1, Pallas kernels: 1.07 us -> 3.05 us  [per_device(): pl.pallas_call(functools.partial(element_kernel, width, early, pairs, own...]
    pallas_call x1, Pallas kernels: 0.93 us -> 2.53 us  [per_device(): pl.pallas_call(functools.partial(gather_kernel, width, early), out_shape=...]
    pallas_call x1, Pallas kernels: 0.86 us -> 2.08 us  [per_device(): pl.pallas_call(functools.partial(scatter_kernel, width), out_shape=[jax.S...]
  transfers between devices with their start and end apart: 8 -> 10, of which waited for: 3 -> 1; matrix products, arithmetic and copies ran while one was open for 0% -> 0% of each run, Pallas kernels for 8% -> 20%
where the time goes in v4:
time: 23.1 us; the launch traced here: 23 us
  starting transfers between devices  10.5 us (45%)
  Pallas kernels  10.2 us (44%)
  waiting for transfers between devices  1.51 us (7%)
  between operations  0.75 us (3%)
    ppermute x10, starting transfers between devices, exchange(): got.append(lax.ppermute(block, AXES, route))  10.5 us
    pallas_call x1, Pallas kernels, per_device(): pl.pallas_call(functools.partial(element_kernel, width, early, pairs, own...  3.05 us
    pallas_call x1, Pallas kernels, per_device(): pl.pallas_call(functools.partial(gather_kernel, width, early), out_shape=...  2.53 us
    pallas_call x1, Pallas kernels, per_device(): pl.pallas_call(functools.partial(scatter_kernel, width), out_shape=[jax.S...  2.08 us
    ppermute x10, waiting for transfers between devices, exchange(): got.append(lax.ppermute(block, AXES, route))  1.51 us
    pallas_call x1, Pallas kernels, per_device(): pl.pallas_call(functools.partial(select_kernel, pairs, len(loads)), out_s...  1.41 us
    pallas_call x1, Pallas kernels, per_device(): pl.pallas_call(functools.partial(finish_kernel, pairs), out_shape=jax.Sha...  1.15 us
  transfers between devices with their start and end apart: 10, of which 1 were waited for; matrix products, arithmetic and copies ran while one was open for 0% of the time, Pallas kernels for 20%

profile of v4, /device:TPU:0, one launch (start us, length us, event | category | flops | bytes accessed | tf_op | source)
XLA Modules:
  0.0 23.0 jit_solution(253429440408767025)
XLA Ops:
  0.0 1.4 %select.1 = (bf16[192,128]{1,0:T(8,128)(2,1)S(1)}, bf16[192,128]{1,0:T(8,128)(2,1)S(1)}, bf16[192,128]{1,0:T(8,128)(2,1)S(1)}, bf16[192,128]{1,0:T(8,128)(2,1)S(...) custom-call(s32[1,4,192]{2,1,0:T(4,128)} %mirror_hbm.1, ...), custom_call_target="tpu_custom_call" | custom-call | flops 100663296 | bytes 1048576 | tf_op jit(solution)/shard_map/select/pallas_call | solution.py:289
  1.4 2.5 %collective-permute-start.4 = (bf16[192,128]{1,0:T(8,128)(2,1)S(1)}, bf16[192,128]{1,0:T(8,128)(2,1)S(1)}, u32[]{:S(2)}, u32[]{:S(2)}) collective-permute-start(bf16[192,128]{1,0:T(8,128)(2,1)S(1)} %get-tuple-element.42), channel_id=1, source_target_pairs={{2,1},{1,0},{0,3},{3,2},{4,5},{6,7},{8,9},{10,11},{12,13},{14,15},... | collective-permute-start | bytes 147464 | tf_op jit(solution)/shard_map/ppermute | solution.py:47
  3.9 0.0 collective-permute-start
  3.9 0.7 %collective-permute-start.1 = (bf16[192,128]{1,0:T(8,128)(2,1)S(1)}, bf16[192,128]{1,0:T(8,128)(2,1)S(1)}, u32[]{:S(2)}, u32[]{:S(2)}) collective-permute-start(bf16[192,128]{1,0:T(8,128)(2,1)S(1)} %get-tuple-element.43), channel_id=1, source_target_pairs={{2,4},{3,5},{6,8},{7,9},{10,12},{11,13},{14,16},{15,17},{18,20},{1... | collective-permute-start | bytes 147464 | tf_op jit(solution)/shard_map/ppermute | solution.py:47
  4.6 2.9 %collective-permute-start.2 = (bf16[192,128]{1,0:T(8,128)(2,1)S(1)}, bf16[192,128]{1,0:T(8,128)(2,1)S(1)}, u32[]{:S(2)}, u32[]{:S(2)}) collective-permute-start(bf16[192,128]{1,0:T(8,128)(2,1)S(1)} %get-tuple-element.44), channel_id=1, source_target_pairs={{0,2},{1,3},{4,6},{5,7},{8,10},{9,11},{12,14},{13,15},{16,18},{17,... | collective-permute-start | bytes 147464 | tf_op jit(solution)/shard_map/ppermute | solution.py:47
  7.5 0.0 collective-permute-start.3
  8.1 2.5 %gather_owned.1 = (f32[128,4096]{1,0:T(8,128)S(1)}, s16[64,4096]{1,0:T(8,128)(2,1)S(1)}, bf16[64,4096]{1,0:T(8,128)(2,1)S(1)}, bf16[768,2048]{1,0:T(8,128)(2,1)S(1)}, bf16[2048,768]{1,0:T(8,128)(2,1)S(1)}) custom-call(s32[1]{0:T(128)S(6)} %copy.10.count_ref, s32[4,4096]{1,0:T(4,128)S(1)} %get-tuple-element.31.index_ref, ...), custom_call_target="tpu_custom_call" | custom-call | flops 4294967296 | bytes 1048576 | tf_op jit(solution)/shard_map/gather_owned/pallas_call | solution.py:312
  10.7 0.0 collective-permute-done.1.rest_1_
  10.7 0.0 collective-permute-done.2.rest_2_
  10.7 0.0 collective-permute-done.3.rest_3_
  10.7 0.0 collective-permute-done.4.rest_4_
  10.7 0.0 collective-permute-done.rest_0_
  10.7 3.0 %elements.1 = (bf16[128,4096]{1,0:T(8,128)(2,1)S(1)}, bf16[192,128]{1,0:T(8,128)(2,1)S(1)}, bf16[192,128]{1,0:T(8,128)(2,1)S(1)}, bf16[192,128]{1,0:T(8,128)(2,1)S(1)}, bf16[192,128]{1,0:T(8,128)(2,1)S(1)}) custom-call(s32[1]{0:T(128)S(6)} %copy.10.count_ref, f32[1,4096]{1,0:T(1,128)S(1)} %get-tuple-element.36.visc_ref, ...), custom_call_target="tpu_custom_call" | custom-call | flops 1610612736 | bytes 1048576 | tf_op jit(solution)/shard_map/elements/pallas_call | solution.py:328
  13.8 0.1 collective-permute-start.9
  13.8 0.5 %collective-permute-start.5 = (bf16[192,128]{1,0:T(8,128)(2,1)S(1)}, bf16[192,128]{1,0:T(8,128)(2,1)S(1)}, u32[]{:S(2)}, u32[]{:S(2)}) collective-permute-start(bf16[192,128]{1,0:T(8,128)(2,1)S(1)} %get-tuple-element.53), channel_id=1, source_target_pairs={{0,1},{1,2},{2,0},{3,4},{5,6},{7,8},{9,10},{11,12},{13,14},{15,16}... | collective-permute-start | bytes 147464 | tf_op jit(solution)/shard_map/ppermute | solution.py:47
  14.3 0.0 collective-permute-start.6
  14.3 3.9 %collective-permute-start.7 = (bf16[192,128]{1,0:T(8,128)(2,1)S(1)}, bf16[192,128]{1,0:T(8,128)(2,1)S(1)}, u32[]{:S(2)}, u32[]{:S(2)}) collective-permute-start(bf16[192,128]{1,0:T(8,128)(2,1)S(1)} %get-tuple-element.55), channel_id=1, source_target_pairs={{0,2},{1,3},{4,6},{5,7},{8,10},{9,11},{12,14},{13,15},{16,18},{17,... | collective-permute-start | bytes 147464 | tf_op jit(solution)/shard_map/ppermute | solution.py:47
  18.2 2.1 %scatter_owned.1 = (f32[512,128]{1,0:T(8,128)S(1)}, bf16[512,192]{1,0:T(8,128)(2,1)S(1)}, bf16[512,192]{1,0:T(8,128)(2,1)S(1)}, bf16[512,192]{1,0:T(8,128)(2,1)S(1)}, bf16[512,192]{1,0:T(8,128)(2,1)S(1)}) custom-call(s32[1]{0:T(128)S(6)} %copy.10.count_ref, s16[64,4096]{1,0:T(8,128)(2,1)S(1)} %get-tuple-element.34.column_ref, ...), custom_call_target="tpu_custom_call" | custom-call | flops 4294967296 | bytes 1048576 | tf_op jit(solution)/shard_map/scatter_owned/pallas_call | solution.py:345
  20.3 0.0 collective-permute-done.6.rest_5_
  20.3 1.5 %collective-permute-done.7.rest_6_ = bf16[192,128]{1,0:T(8,128)(2,1)S(1)} collective-permute-done((bf16[192,128]{1,0:T(8,128)(2,1)S(1)}, bf16[192,128]{1,0:T(8,128)(2,1)S(1)}, u32[]{:S(2)}, u32[]{:S(2)}) %collective-permute-start.7) | collective-permute-done | bytes 49184 | tf_op jit(solution)/shard_map/ppermute | solution.py:47
  21.8 0.0 collective-permute-done.8.rest_7_
  21.8 0.0 collective-permute-done.9.rest_8_
  21.8 0.0 collective-permute-done.5.rest_4_
  21.8 1.1 %finish.1 = f32[512,128]{1,0:T(8,128)} custom-call(f32[512,128]{1,0:T(8,128)S(1)} %get-tuple-element.48.part_ref, bf16[512,192]{1,0:T(8,128)(2,1)S(1)} %get-tuple-element.49.rest_0_, bf16[512,192]{1,0:T(8,128)(2,1)S(1)} %get-tuple-element.50.rest_1_, bf16[512,192]{1,0:T(8,128)(2,1)S(1)} %get-tuple-element.51.rest_2_, ...), custom_call_target="tpu_custom_call" | custom-call | flops 100663296 | bytes 1048576 | tf_op jit(solution)/shard_map/finish/pallas_call | solution.py:356
  (1 shorter events, 0.0 us)
Async XLA Ops:
  1.4 9.3 %collective-permute-start.4 = (bf16[192,128]{1,0:T(8,128)(2,1)S(1)}, bf16[192,128]{1,0:T(8,128)(2,1)S(1)}, u32[]{:S(2)}, u32[]{:S(2)}) collective-permute-start(bf16[192,128]{1,0:T(8,128)(2,1)S(1)} %get-tuple-element.42), channel_id=1, source_target_pairs={{2,1},{1,0},{0,3},{3,2},{4,5},{6,7},{8,9},{10,11},{12,13},{14,15},... | collective-permute-start | bytes 147464 | tf_op jit(solution)/shard_map/ppermute | solution.py:47
  3.9 6.8 %collective-permute-start = (bf16[192,128]{1,0:T(8,128)(2,1)S(1)}, bf16[192,128]{1,0:T(8,128)(2,1)S(1)}, u32[]{:S(2)}, u32[]{:S(2)}) collective-permute-start(bf16[192,128]{1,0:T(8,128)(2,1)S(1)} %get-tuple-element.42), channel_id=1, source_target_pairs={{0,1},{1,2},{2,0},{3,4},{5,6},{7,8},{9,10},{11,12},{13,14},{15,16}... | collective-permute-start | bytes 147464 | tf_op jit(solution)/shard_map/ppermute | solution.py:47
  3.9 6.8 %collective-permute-start.1 = (bf16[192,128]{1,0:T(8,128)(2,1)S(1)}, bf16[192,128]{1,0:T(8,128)(2,1)S(1)}, u32[]{:S(2)}, u32[]{:S(2)}) collective-permute-start(bf16[192,128]{1,0:T(8,128)(2,1)S(1)} %get-tuple-element.43), channel_id=1, source_target_pairs={{2,4},{3,5},{6,8},{7,9},{10,12},{11,13},{14,16},{15,17},{18,20},{1... | collective-permute-start | bytes 147464 | tf_op jit(solution)/shard_map/ppermute | solution.py:47
  4.6 6.1 %collective-permute-start.2 = (bf16[192,128]{1,0:T(8,128)(2,1)S(1)}, bf16[192,128]{1,0:T(8,128)(2,1)S(1)}, u32[]{:S(2)}, u32[]{:S(2)}) collective-permute-start(bf16[192,128]{1,0:T(8,128)(2,1)S(1)} %get-tuple-element.44), channel_id=1, source_target_pairs={{0,2},{1,3},{4,6},{5,7},{8,10},{9,11},{12,14},{13,15},{16,18},{17,... | collective-permute-start | bytes 147464 | tf_op jit(solution)/shard_map/ppermute | solution.py:47
  7.5 3.2 %collective-permute-start.3 = (bf16[192,128]{1,0:T(8,128)(2,1)S(1)}, bf16[192,128]{1,0:T(8,128)(2,1)S(1)}, u32[]{:S(2)}, u32[]{:S(2)}) collective-permute-start(bf16[192,128]{1,0:T(8,128)(2,1)S(1)} %get-tuple-element.45), channel_id=1, source_target_pairs={{0,1},{2,3},{4,5},{6,7},{8,9},{10,11},{12,13},{14,15},{16,17},{18,... | collective-permute-start | bytes 147464 | tf_op jit(solution)/shard_map/ppermute | solution.py:47
  13.8 8.0 %collective-permute-start.9 = (bf16[192,128]{1,0:T(8,128)(2,1)S(1)}, bf16[192,128]{1,0:T(8,128)(2,1)S(1)}, u32[]{:S(2)}, u32[]{:S(2)}) collective-permute-start(bf16[192,128]{1,0:T(8,128)(2,1)S(1)} %get-tuple-element.53), channel_id=1, source_target_pairs={{2,1},{1,0},{0,3},{3,2},{4,5},{6,7},{8,9},{10,11},{12,13},{14,15},... | collective-permute-start | bytes 147464 | tf_op jit(solution)/shard_map/ppermute | solution.py:47
  13.8 8.0 %collective-permute-start.5 = (bf16[192,128]{1,0:T(8,128)(2,1)S(1)}, bf16[192,128]{1,0:T(8,128)(2,1)S(1)}, u32[]{:S(2)}, u32[]{:S(2)}) collective-permute-start(bf16[192,128]{1,0:T(8,128)(2,1)S(1)} %get-tuple-element.53), channel_id=1, source_target_pairs={{0,1},{1,2},{2,0},{3,4},{5,6},{7,8},{9,10},{11,12},{13,14},{15,16}... | collective-permute-start | bytes 147464 | tf_op jit(solution)/shard_map/ppermute | solution.py:47
  14.3 6.0 %collective-permute-start.6 = (bf16[192,128]{1,0:T(8,128)(2,1)S(1)}, bf16[192,128]{1,0:T(8,128)(2,1)S(1)}, u32[]{:S(2)}, u32[]{:S(2)}) collective-permute-start(bf16[192,128]{1,0:T(8,128)(2,1)S(1)} %get-tuple-element.54), channel_id=1, source_target_pairs={{2,4},{3,5},{6,8},{7,9},{10,12},{11,13},{14,16},{15,17},{18,20},{1... | collective-permute-start | bytes 147464 | tf_op jit(solution)/shard_map/ppermute | solution.py:47
  14.3 7.5 %collective-permute-start.7 = (bf16[192,128]{1,0:T(8,128)(2,1)S(1)}, bf16[192,128]{1,0:T(8,128)(2,1)S(1)}, u32[]{:S(2)}, u32[]{:S(2)}) collective-permute-start(bf16[192,128]{1,0:T(8,128)(2,1)S(1)} %get-tuple-element.55), channel_id=1, source_target_pairs={{0,2},{1,3},{4,6},{5,7},{8,10},{9,11},{12,14},{13,15},{16,18},{17,... | collective-permute-start | bytes 147464 | tf_op jit(solution)/shard_map/ppermute | solution.py:47
  18.2 3.6 %collective-permute-start.8 = (bf16[192,128]{1,0:T(8,128)(2,1)S(1)}, bf16[192,128]{1,0:T(8,128)(2,1)S(1)}, u32[]{:S(2)}, u32[]{:S(2)}) collective-permute-start(bf16[192,128]{1,0:T(8,128)(2,1)S(1)} %get-tuple-element.56), channel_id=1, source_target_pairs={{0,1},{2,3},{4,5},{6,7},{8,9},{10,11},{12,13},{14,15},{16,17},{18,... | collective-permute-start | bytes 147464 | tf_op jit(solution)/shard_map/ppermute | solution.py:47

commit v5 on v4

--- a/solution.py
+++ b/solution.py
@@ -73,7 +73,7 @@
 
 
 def transposed(values):
-    return values.astype(jnp.float32).T.astype(jnp.bfloat16)
+    return values.astype(jnp.bfloat16).T
 
 
 def matmul(a, b):
@@ -109,7 +109,7 @@
         region, there = send_region(distance, parity)
         names = jnp.where(lane < jnp.where(there, live_ref[0, region], 0), mirror_ref[0, pl.ds(region, 1), :], -1)
         names_ref[pl.ds(m, 1), :] = names
-        sent_refs[m][...] = matmul(flipped, one_hot(names, rows)).T.astype(jnp.bfloat16)
+        sent_refs[m][...] = transposed(matmul(flipped, one_hot(names, rows)))
     for copy in later:
         copy.wait()
 
@@ -199,7 +199,7 @@
 
     def work(total):
         flipped = transposed(ghost_all[...])
-        both = jnp.concatenate([mats_v_ref[...].astype(jnp.float32).T, mats_p_ref[...].astype(jnp.float32).T], axis=1).astype(jnp.bfloat16)
+        both = jnp.concatenate([mats_v_ref[...].T, mats_p_ref[...].T], axis=1)
         blocks = spans(total, width)
         for lanes in blocks:
             ein = ein_ref[:, lanes]
@@ -219,9 +219,9 @@
         summed = matmul(out_ref[:, :first], turned_ref[:first, :])
         if total > early:
             summed = summed + matmul(out_ref[:, early:total], late_ref[: total - early, :])
-        back[...] = summed.T
+        back[...] = transposed(summed)
         for spot, ret_ref in zip(spots, ret_refs):
-            ret_ref[...] = back[spot, :].astype(jnp.bfloat16)
+            ret_ref[...] = back[spot, :]
 
     by_load(count_ref[0], ein_ref.shape[1], work)
 
@@ -334,7 +334,7 @@
             pltpu.VMEM((regions * ghost, channels), bf16),
             pltpu.VMEM((2 * channels, elements), bf16),
             pltpu.VMEM((max(elements - early, PACK), regions * ghost), bf16),
-            pltpu.VMEM((regions * ghost, channels), f32),
+            pltpu.VMEM((regions * ghost, channels), bf16),
         ],
         compiler_params=params(24),
         cost_estimate=cost(table_flops * regions * ghost * 2),

time: 23.1 us -> 23.1 us (level)
  no operation moved by 1% of the time
where the time goes in v5:
time: 23.1 us; the launch traced here: 22.9 us
  starting transfers between devices  10.5 us (45%)
  Pallas kernels  10.2 us (44%)
  waiting for transfers between devices  1.51 us (7%)
  between operations  0.75 us (3%)
    ppermute x10, starting transfers between devices, exchange(): got.append(lax.ppermute(block, AXES, route))  10.5 us
    pallas_call x1, Pallas kernels, per_device(): pl.pallas_call(functools.partial(element_kernel, width, early, pairs, own...  3 us
    pallas_call x1, Pallas kernels, per_device(): pl.pallas_call(functools.partial(gather_kernel, width, early), out_shape=...  2.53 us
    pallas_call x1, Pallas kernels, per_device(): pl.pallas_call(functools.partial(scatter_kernel, width), out_shape=[jax.S...  2.08 us
    ppermute x10, waiting for transfers between devices, exchange(): got.append(lax.ppermute(block, AXES, route))  1.51 us
    pallas_call x1, Pallas kernels, per_device(): pl.pallas_call(functools.partial(select_kernel, pairs, len(loads)), out_s...  1.4 us
    pallas_call x1, Pallas kernels, per_device(): pl.pallas_call(functools.partial(finish_kernel, pairs), out_shape=jax.Sha...  1.15 us
  transfers between devices with their start and end apart: 10, of which 1 were waited for; matrix products, arithmetic and copies ran while one was open for 0% of the time, Pallas kernels for 20%

profile of v5, /device:TPU:0, one launch (start us, length us, event | category | flops | bytes accessed | tf_op | source)
XLA Modules:
  0.0 22.9 jit_solution(12922246876362745788)
XLA Ops:
  0.0 1.4 %select.1 = (bf16[192,128]{1,0:T(8,128)(2,1)S(1)}, bf16[192,128]{1,0:T(8,128)(2,1)S(1)}, bf16[192,128]{1,0:T(8,128)(2,1)S(1)}, bf16[192,128]{1,0:T(8,128)(2,1)S(...) custom-call(s32[1,4,192]{2,1,0:T(4,128)} %mirror_hbm.1, ...), custom_call_target="tpu_custom_call" | custom-call | flops 100663296 | bytes 1048576 | tf_op jit(solution)/shard_map/select/pallas_call | solution.py:289
  1.4 2.5 %collective-permute-start.4 = (bf16[192,128]{1,0:T(8,128)(2,1)S(1)}, bf16[192,128]{1,0:T(8,128)(2,1)S(1)}, u32[]{:S(2)}, u32[]{:S(2)}) collective-permute-start(bf16[192,128]{1,0:T(8,128)(2,1)S(1)} %get-tuple-element.42), channel_id=1, source_target_pairs={{2,1},{1,0},{0,3},{3,2},{4,5},{6,7},{8,9},{10,11},{12,13},{14,15},... | collective-permute-start | bytes 147464 | tf_op jit(solution)/shard_map/ppermute | solution.py:47
  3.9 0.0 collective-permute-start
  3.9 0.7 %collective-permute-start.1 = (bf16[192,128]{1,0:T(8,128)(2,1)S(1)}, bf16[192,128]{1,0:T(8,128)(2,1)S(1)}, u32[]{:S(2)}, u32[]{:S(2)}) collective-permute-start(bf16[192,128]{1,0:T(8,128)(2,1)S(1)} %get-tuple-element.43), channel_id=1, source_target_pairs={{2,4},{3,5},{6,8},{7,9},{10,12},{11,13},{14,16},{15,17},{18,20},{1... | collective-permute-start | bytes 147464 | tf_op jit(solution)/shard_map/ppermute | solution.py:47
  4.6 2.9 %collective-permute-start.2 = (bf16[192,128]{1,0:T(8,128)(2,1)S(1)}, bf16[192,128]{1,0:T(8,128)(2,1)S(1)}, u32[]{:S(2)}, u32[]{:S(2)}) collective-permute-start(bf16[192,128]{1,0:T(8,128)(2,1)S(1)} %get-tuple-element.44), channel_id=1, source_target_pairs={{0,2},{1,3},{4,6},{5,7},{8,10},{9,11},{12,14},{13,15},{16,18},{17,... | collective-permute-start | bytes 147464 | tf_op jit(solution)/shard_map/ppermute | solution.py:47
  7.5 0.0 collective-permute-start.3
  8.1 2.5 %gather_owned.1 = (f32[128,4096]{1,0:T(8,128)S(1)}, s16[64,4096]{1,0:T(8,128)(2,1)S(1)}, bf16[64,4096]{1,0:T(8,128)(2,1)S(1)}, bf16[768,2048]{1,0:T(8,128)(2,1)S(1)}, bf16[2048,768]{1,0:T(8,128)(2,1)S(1)}) custom-call(s32[1]{0:T(128)S(6)} %copy.10.count_ref, s32[4,4096]{1,0:T(4,128)S(1)} %get-tuple-element.31.index_ref, ...), custom_call_target="tpu_custom_call" | custom-call | flops 4294967296 | bytes 1048576 | tf_op jit(solution)/shard_map/gather_owned/pallas_call | solution.py:312
  10.7 0.0 collective-permute-done.1.rest_1_
  10.7 0.0 collective-permute-done.2.rest_2_
  10.7 0.0 collective-permute-done.3.rest_3_
  10.7 0.0 collective-permute-done.4.rest_4_
  10.7 0.0 collective-permute-done.rest_0_
  10.7 3.0 %elements.1 = (bf16[128,4096]{1,0:T(8,128)(2,1)S(1)}, bf16[192,128]{1,0:T(8,128)(2,1)S(1)}, bf16[192,128]{1,0:T(8,128)(2,1)S(1)}, bf16[192,128]{1,0:T(8,128)(2,1)S(1)}, bf16[192,128]{1,0:T(8,128)(2,1)S(1)}) custom-call(s32[1]{0:T(128)S(6)} %copy.10.count_ref, f32[1,4096]{1,0:T(1,128)S(1)} %get-tuple-element.36.visc_ref, ...), custom_call_target="tpu_custom_call" | custom-call | flops 1610612736 | bytes 1048576 | tf_op jit(solution)/shard_map/elements/pallas_call | solution.py:328
  13.7 0.1 collective-permute-start.9
  13.8 0.5 %collective-permute-start.5 = (bf16[192,128]{1,0:T(8,128)(2,1)S(1)}, bf16[192,128]{1,0:T(8,128)(2,1)S(1)}, u32[]{:S(2)}, u32[]{:S(2)}) collective-permute-start(bf16[192,128]{1,0:T(8,128)(2,1)S(1)} %get-tuple-element.53), channel_id=1, source_target_pairs={{0,1},{1,2},{2,0},{3,4},{5,6},{7,8},{9,10},{11,12},{13,14},{15,16}... | collective-permute-start | bytes 147464 | tf_op jit(solution)/shard_map/ppermute | solution.py:47
  14.3 0.0 collective-permute-start.6
  14.3 3.9 %collective-permute-start.7 = (bf16[192,128]{1,0:T(8,128)(2,1)S(1)}, bf16[192,128]{1,0:T(8,128)(2,1)S(1)}, u32[]{:S(2)}, u32[]{:S(2)}) collective-permute-start(bf16[192,128]{1,0:T(8,128)(2,1)S(1)} %get-tuple-element.55), channel_id=1, source_target_pairs={{0,2},{1,3},{4,6},{5,7},{8,10},{9,11},{12,14},{13,15},{16,18},{17,... | collective-permute-start | bytes 147464 | tf_op jit(solution)/shard_map/ppermute | solution.py:47
  18.2 2.1 %scatter_owned.1 = (f32[512,128]{1,0:T(8,128)S(1)}, bf16[512,192]{1,0:T(8,128)(2,1)S(1)}, bf16[512,192]{1,0:T(8,128)(2,1)S(1)}, bf16[512,192]{1,0:T(8,128)(2,1)S(1)}, bf16[512,192]{1,0:T(8,128)(2,1)S(1)}) custom-call(s32[1]{0:T(128)S(6)} %copy.10.count_ref, s16[64,4096]{1,0:T(8,128)(2,1)S(1)} %get-tuple-element.34.column_ref, ...), custom_call_target="tpu_custom_call" | custom-call | flops 4294967296 | bytes 1048576 | tf_op jit(solution)/shard_map/scatter_owned/pallas_call | solution.py:345
  20.3 0.0 collective-permute-done.6.rest_5_
  20.3 1.5 %collective-permute-done.7.rest_6_ = bf16[192,128]{1,0:T(8,128)(2,1)S(1)} collective-permute-done((bf16[192,128]{1,0:T(8,128)(2,1)S(1)}, bf16[192,128]{1,0:T(8,128)(2,1)S(1)}, u32[]{:S(2)}, u32[]{:S(2)}) %collective-permute-start.7) | collective-permute-done | bytes 49184 | tf_op jit(solution)/shard_map/ppermute | solution.py:47
  21.8 0.0 collective-permute-done.8.rest_7_
  21.8 0.0 collective-permute-done.9.rest_8_
  21.8 0.0 collective-permute-done.5.rest_4_
  21.8 1.1 %finish.1 = f32[512,128]{1,0:T(8,128)} custom-call(f32[512,128]{1,0:T(8,128)S(1)} %get-tuple-element.48.part_ref, bf16[512,192]{1,0:T(8,128)(2,1)S(1)} %get-tuple-element.49.rest_0_, bf16[512,192]{1,0:T(8,128)(2,1)S(1)} %get-tuple-element.50.rest_1_, bf16[512,192]{1,0:T(8,128)(2,1)S(1)} %get-tuple-element.51.rest_2_, ...), custom_call_target="tpu_custom_call" | custom-call | flops 100663296 | bytes 1048576 | tf_op jit(solution)/shard_map/finish/pallas_call | solution.py:356
  (1 shorter events, 0.0 us)
Async XLA Ops:
  1.4 9.3 %collective-permute-start.4 = (bf16[192,128]{1,0:T(8,128)(2,1)S(1)}, bf16[192,128]{1,0:T(8,128)(2,1)S(1)}, u32[]{:S(2)}, u32[]{:S(2)}) collective-permute-start(bf16[192,128]{1,0:T(8,128)(2,1)S(1)} %get-tuple-element.42), channel_id=1, source_target_pairs={{2,1},{1,0},{0,3},{3,2},{4,5},{6,7},{8,9},{10,11},{12,13},{14,15},... | collective-permute-start | bytes 147464 | tf_op jit(solution)/shard_map/ppermute | solution.py:47
  3.9 6.8 %collective-permute-start = (bf16[192,128]{1,0:T(8,128)(2,1)S(1)}, bf16[192,128]{1,0:T(8,128)(2,1)S(1)}, u32[]{:S(2)}, u32[]{:S(2)}) collective-permute-start(bf16[192,128]{1,0:T(8,128)(2,1)S(1)} %get-tuple-element.42), channel_id=1, source_target_pairs={{0,1},{1,2},{2,0},{3,4},{5,6},{7,8},{9,10},{11,12},{13,14},{15,16}... | collective-permute-start | bytes 147464 | tf_op jit(solution)/shard_map/ppermute | solution.py:47
  3.9 6.8 %collective-permute-start.1 = (bf16[192,128]{1,0:T(8,128)(2,1)S(1)}, bf16[192,128]{1,0:T(8,128)(2,1)S(1)}, u32[]{:S(2)}, u32[]{:S(2)}) collective-permute-start(bf16[192,128]{1,0:T(8,128)(2,1)S(1)} %get-tuple-element.43), channel_id=1, source_target_pairs={{2,4},{3,5},{6,8},{7,9},{10,12},{11,13},{14,16},{15,17},{18,20},{1... | collective-permute-start | bytes 147464 | tf_op jit(solution)/shard_map/ppermute | solution.py:47
  4.6 6.1 %collective-permute-start.2 = (bf16[192,128]{1,0:T(8,128)(2,1)S(1)}, bf16[192,128]{1,0:T(8,128)(2,1)S(1)}, u32[]{:S(2)}, u32[]{:S(2)}) collective-permute-start(bf16[192,128]{1,0:T(8,128)(2,1)S(1)} %get-tuple-element.44), channel_id=1, source_target_pairs={{0,2},{1,3},{4,6},{5,7},{8,10},{9,11},{12,14},{13,15},{16,18},{17,... | collective-permute-start | bytes 147464 | tf_op jit(solution)/shard_map/ppermute | solution.py:47
  7.5 3.2 %collective-permute-start.3 = (bf16[192,128]{1,0:T(8,128)(2,1)S(1)}, bf16[192,128]{1,0:T(8,128)(2,1)S(1)}, u32[]{:S(2)}, u32[]{:S(2)}) collective-permute-start(bf16[192,128]{1,0:T(8,128)(2,1)S(1)} %get-tuple-element.45), channel_id=1, source_target_pairs={{0,1},{2,3},{4,5},{6,7},{8,9},{10,11},{12,13},{14,15},{16,17},{18,... | collective-permute-start | bytes 147464 | tf_op jit(solution)/shard_map/ppermute | solution.py:47
  13.7 8.0 %collective-permute-start.9 = (bf16[192,128]{1,0:T(8,128)(2,1)S(1)}, bf16[192,128]{1,0:T(8,128)(2,1)S(1)}, u32[]{:S(2)}, u32[]{:S(2)}) collective-permute-start(bf16[192,128]{1,0:T(8,128)(2,1)S(1)} %get-tuple-element.53), channel_id=1, source_target_pairs={{2,1},{1,0},{0,3},{3,2},{4,5},{6,7},{8,9},{10,11},{12,13},{14,15},... | collective-permute-start | bytes 147464 | tf_op jit(solution)/shard_map/ppermute | solution.py:47
  13.8 8.0 %collective-permute-start.5 = (bf16[192,128]{1,0:T(8,128)(2,1)S(1)}, bf16[192,128]{1,0:T(8,128)(2,1)S(1)}, u32[]{:S(2)}, u32[]{:S(2)}) collective-permute-start(bf16[192,128]{1,0:T(8,128)(2,1)S(1)} %get-tuple-element.53), channel_id=1, source_target_pairs={{0,1},{1,2},{2,0},{3,4},{5,6},{7,8},{9,10},{11,12},{13,14},{15,16}... | collective-permute-start | bytes 147464 | tf_op jit(solution)/shard_map/ppermute | solution.py:47
  14.3 6.0 %collective-permute-start.6 = (bf16[192,128]{1,0:T(8,128)(2,1)S(1)}, bf16[192,128]{1,0:T(8,128)(2,1)S(1)}, u32[]{:S(2)}, u32[]{:S(2)}) collective-permute-start(bf16[192,128]{1,0:T(8,128)(2,1)S(1)} %get-tuple-element.54), channel_id=1, source_target_pairs={{2,4},{3,5},{6,8},{7,9},{10,12},{11,13},{14,16},{15,17},{18,20},{1... | collective-permute-start | bytes 147464 | tf_op jit(solution)/shard_map/ppermute | solution.py:47
  14.3 7.5 %collective-permute-start.7 = (bf16[192,128]{1,0:T(8,128)(2,1)S(1)}, bf16[192,128]{1,0:T(8,128)(2,1)S(1)}, u32[]{:S(2)}, u32[]{:S(2)}) collective-permute-start(bf16[192,128]{1,0:T(8,128)(2,1)S(1)} %get-tuple-element.55), channel_id=1, source_target_pairs={{0,2},{1,3},{4,6},{5,7},{8,10},{9,11},{12,14},{13,15},{16,18},{17,... | collective-permute-start | bytes 147464 | tf_op jit(solution)/shard_map/ppermute | solution.py:47
  18.2 3.6 %collective-permute-start.8 = (bf16[192,128]{1,0:T(8,128)(2,1)S(1)}, bf16[192,128]{1,0:T(8,128)(2,1)S(1)}, u32[]{:S(2)}, u32[]{:S(2)}) collective-permute-start(bf16[192,128]{1,0:T(8,128)(2,1)S(1)} %get-tuple-element.56), channel_id=1, source_target_pairs={{0,1},{2,3},{4,5},{6,7},{8,9},{10,11},{12,13},{14,15},{16,17},{18,... | collective-permute-start | bytes 147464 | tf_op jit(solution)/shard_map/ppermute | solution.py:47
